TPU v7x, 8 devices: a whole 2x2x1 slice. The times are simulated.
8 devices in a mesh: dp: 1 (over z), tp: 2 (over y), cp: 4 (over x, core).
Axes of the slice: x: 2, y: 2, z: 1, core: 2. Of those that a mesh axis runs over, the one named last changes fastest.
Arguments:
- hidden: bfloat16 [24, 64, 2048], P('dp')
- attn_gain: bfloat16 [2048], replicated
- w_query: bfloat16 [2048, 2048], P(None, 'tp')
- w_key: bfloat16 [2048, 512], P(None, 'tp')
- w_value: bfloat16 [2048, 512], P(None, 'tp')
- w_out: bfloat16 [2048, 2048], P('tp')
- cache_k: bfloat16 [24, 4, 4, 8, 256, 64], P('dp', None, 'cp', 'tp')
- cache_v: bfloat16 [24, 4, 4, 8, 256, 64], P('dp', None, 'cp', 'tp')
- ctx_len: int32 [24], P('dp')
- positions: int32 [24, 64], P('dp')
- tree_mask: int32 [24, 64, 64], P('dp')
Outputs:
- output 1: bfloat16 [24, 64, 2048], P('dp')
- output 2: bfloat16 [24, 4, 4, 8, 256, 64], P('dp', None, 'cp', 'tp')
- output 3: bfloat16 [24, 4, 4, 8, 256, 64], P('dp', None, 'cp', 'tp')
All inputs are finite; a program needn't handle non-finite values.
Results may differ from a plain program's by a relative error of at most 0.00876036.
Values sent between devices are 32-bit elements.
A program may use at most 1 GiB of HBM per device.

v0:
```python
import functools
import math
import jax
import jax.numpy as jnp
from jax import lax
from jax.experimental import pallas as pl
from jax.experimental.pallas import tpu as pltpu
from jax.sharding import PartitionSpec as P

ROPE_THETA = 500000.0
NORM_EPS = 1e-5
MASKED = -1e30
LOG2E = math.log2(math.e)
MESH = pl.DeviceIdType.MESH
F32 = jnp.float32
BF16 = jnp.bfloat16
CHUNK = 4


def mm(a, b):
    return jnp.dot(a, b, preferred_element_type=F32)


def mm_tn(a, b):
    return lax.dot_general(a, b, (((0,), (0,)), ((), ())), preferred_element_type=F32)


def rope_tables(positions, head_dim):
    freq_idx = jnp.arange(head_dim // 2, dtype=F32)
    inv_freq = 1.0 / (ROPE_THETA ** (2.0 * freq_idx / head_dim))
    wavelen = 2.0 * math.pi / inv_freq
    smooth = (8192.0 / wavelen - 1.0) / 3.0
    blended = (1.0 - smooth) * inv_freq / 8.0 + smooth * inv_freq
    inv_freq = jnp.where(wavelen < 2048.0, inv_freq, jnp.where(wavelen > 8192.0, inv_freq / 8.0, blended))
    angle = positions.astype(F32)[:, None, :] * inv_freq[None, :, None]
    return jnp.cos(angle), jnp.sin(angle)


def qkv_kernel(ctx_ref, x_ref, gain_ref, wq_ref, wk_ref, wv_ref, cos_ref, sin_ref, kc_hbm, vc_hbm,
               q_ref, ko_hbm, vo_hbm, buf, new_ref, in_sem, out_sem):
    step, steps = pl.program_id(0), pl.num_programs(0)
    cp_rank, cp_size = lax.axis_index('cp'), lax.axis_size('cp')
    slot = lax.rem(step, 2)
    num_blocks, kv_heads, hd, blk = buf.shape[3:]
    half = hd // 2
    tree = x_ref.shape[0] // CHUNK
    heads = q_ref.shape[1]
    group = q_ref.shape[3] // tree

    def fetch(idx, to):
        rows = pl.ds(idx * CHUNK, CHUNK)
        return [pltpu.make_async_copy(src.at[rows], buf.at[to, n], in_sem.at[to, n]) for n, src in enumerate((kc_hbm, vc_hbm))]

    def flush(idx, frm):
        rows = pl.ds(idx * CHUNK, CHUNK)
        return [pltpu.make_async_copy(buf.at[frm, n], dst.at[rows], out_sem.at[frm, n]) for n, dst in enumerate((ko_hbm, vo_hbm))]

    @pl.when(step == 0)
    def _():
        for c in fetch(0, 0):
            c.start()

    @pl.when(step >= 1)
    def _():
        for c in flush(step - 1, 1 - slot):
            c.wait()

    @pl.when(step + 1 < steps)
    def _():
        for c in fetch(step + 1, 1 - slot):
            c.start()

    wide = x_ref[...].astype(F32)
    inv_rms = lax.rsqrt(jnp.mean(wide * wide, axis=-1, keepdims=True) + NORM_EPS)
    h = (wide * inv_rms * gain_ref[...].astype(F32)).astype(BF16)
    cos, sin = cos_ref[0], sin_ref[0]

    def rotate(rows):
        first, second = rows[:half], rows[half:]
        return jnp.concatenate([first * cos - second * sin, second * cos + first * sin], axis=0)

    key_t = mm(h, wk_ref[...]).T
    for n in range(kv_heads):
        new_ref[0, n * hd:(n + 1) * hd, :] = rotate(key_t[n * hd:(n + 1) * hd]).astype(BF16)
    new_ref[1] = mm(h, wv_ref[...]).T.astype(BF16)

    for c in fetch(step, slot):
        c.wait()
    cols = CHUNK * tree
    for i in range(CHUNK):
        ctx = ctx_ref[step * CHUNK + i]
        for j in range(num_blocks // 2, num_blocks):
            first_pos = (j * cp_size + cp_rank) * blk

            @pl.when((first_pos < ctx + tree) & (first_pos + blk > ctx))
            def _():
                tok = first_pos - ctx + lax.broadcasted_iota(jnp.int32, (cols, blk), 1)
                row = lax.broadcasted_iota(jnp.int32, (cols, blk), 0) - i * tree
                pick = jnp.where((row == tok) & (row >= 0) & (row < tree), 1.0, 0.0).astype(BF16)
                tok_h = first_pos - ctx + lax.broadcasted_iota(jnp.int32, (hd, blk), 1)
                fresh = (tok_h >= 0) & (tok_h < tree)
                for n in range(2):
                    put = mm(new_ref[n], pick)
                    for head in range(kv_heads):
                        old = buf[slot, n, i, j, head].astype(F32)
                        buf[slot, n, i, j, head] = jnp.where(fresh, put[head * hd:(head + 1) * hd], old).astype(BF16)

    for c in flush(step, slot):
        c.start()
    for head in range(heads):
        cols_h = pl.ds(head * group * hd, group * hd)
        q_t = mm(h, wq_ref[:, cols_h]).T
        parts = [rotate(q_t[g * hd:(g + 1) * hd]) for g in range(group)]
        for i in range(CHUNK):
            q_ref[i, head] = jnp.concatenate([p[:, i * tree:(i + 1) * tree] for p in parts], axis=1).astype(BF16)

    @pl.when(step == steps - 1)
    def _():
        for c in flush(step, slot):
            c.wait()


def attend_kernel(ctx_ref, q_ref, bias_ref, kc_hbm, vc_hbm, hid_hbm, wo_hbm, y_ref,
                  kbuf, vbuf, kext, qext, scores, msg, rpart, xsend, xrecv, psend, precv, wout, resid,
                  kv_sem, w_sem, hid_sem, snd, rcv):
    cp, tp = lax.axis_index('cp'), lax.axis_index('tp')
    chip, core = cp // 2, cp % 2
    partner = {'cp': chip * 2 + 1 - core}
    across_x = {'cp': (1 - chip) * 2 + core}
    across_y = {'tp': 1 - tp}
    heads, hd, qcols = q_ref.shape[1:]
    tree = bias_ref.shape[1]
    group = qcols // tree
    num_blocks, blk = kbuf.shape[1], kbuf.shape[4]
    nreq = q_ref.shape[0]
    chunks = nreq // CHUNK
    width = wo_hbm.shape[1]
    wcols = width // 2
    coef = hd ** -0.5 * LOG2E
    own_cols = pl.ds(pl.multiple_of(tp * wcols, wcols), wcols)
    other_cols = pl.ds(pl.multiple_of((1 - tp) * wcols, wcols), wcols)

    def remote(src, dst, k, n, to):
        return pltpu.make_async_remote_copy(src_ref=src, dst_ref=dst, send_sem=snd.at[k, n], recv_sem=rcv.at[k, n], device_id=to, device_id_type=MESH)

    barrier = pltpu.get_barrier_semaphore()
    for to in (partner, across_x, across_y):
        pl.semaphore_signal(barrier, inc=1, device_id=to, device_id_type=MESH)

    def request_of(n):
        return (n // CHUNK) * CHUNK + (2 * (1 - chip) + n % CHUNK) % CHUNK

    def fetch(n):
        r, to = request_of(n), n % 2
        return [pltpu.make_async_copy(kc_hbm.at[r], kbuf.at[to], kv_sem.at[to, 0]),
                pltpu.make_async_copy(vc_hbm.at[r], vbuf.at[to, :, :, pl.ds(0, hd), :], kv_sem.at[to, 1])]

    def weight_copies():
        out = []
        for g in range(group):
            for h in range(heads):
                out.append(pltpu.make_async_copy(wo_hbm.at[pl.ds((h * group + g) * hd, hd)], wout.at[g, pl.ds(h * hd, hd)], w_sem.at[g, h]))
        return out

    def resid_copies():
        return [pltpu.make_async_copy(hid_hbm.at[k * CHUNK + cp, :, own_cols], resid.at[k], hid_sem.at[k]) for k in range(chunks)]

    for c in fetch(0):
        c.start()
    for c in weight_copies() + resid_copies():
        c.start()
    ones = jnp.ones((vbuf.shape[3] - hd, blk), BF16)
    for s in range(2):
        for j in range(num_blocks):
            for h in range(heads):
                vbuf[s, j, h, hd:, :] = ones
    pad = qext.shape[1] - hd - tree
    hide = jnp.where(lax.broadcasted_iota(jnp.int32, (pad, qcols), 0) == 0, MASKED, 0.0).astype(BF16)
    for h in range(heads):
        qext[h, hd + tree:, :] = hide
    pl.semaphore_wait(barrier, 3)
    for c in weight_copies() + resid_copies():
        c.wait()

    def attend(n):
        k, r, slot = n // CHUNK, request_of(n), n % 2
        i = r - k * CHUNK

        @pl.when(n + 1 < nreq)
        def _():
            for c in fetch(n + 1):
                c.start()

        ctx = ctx_ref[r]
        bias = bias_ref[r]
        for h in range(heads):
            qext[h, :hd, :] = q_ref[r, h]
            qext[h, hd:hd + tree, :] = bias
        for c in fetch(n):
            c.wait()
        late = num_blocks // 2
        for j in range(late, num_blocks):
            off = (j * 4 + cp) * blk - ctx
            tok = off + lax.broadcasted_iota(jnp.int32, (tree, blk), 1)
            pick = jnp.where(tok == lax.broadcasted_iota(jnp.int32, (tree, blk), 0), 1.0, 0.0).astype(BF16)
            tok_p = off + lax.broadcasted_iota(jnp.int32, (pad, blk), 1)
            tail = jnp.where((tok_p >= tree) & (lax.broadcasted_iota(jnp.int32, (pad, blk), 0) == 0), 1.0, 0.0).astype(BF16)
            tok_h = off + lax.broadcasted_iota(jnp.int32, (hd, blk), 1)
            for h in range(heads):
                kext[j - late, h, :hd, :] = jnp.where(tok_h < tree, kbuf[slot, j, h].astype(F32), 0.0).astype(BF16)
                kext[j - late, h, hd:hd + tree, :] = pick
                kext[j - late, h, hd + tree:, :] = tail

        def score(h, j):
            if j < late:
                s = mm_tn(kbuf[slot, j, h], qext[h, :hd, :])
            else:
                s = mm_tn(kext[j - late, h], qext[h])
            scores[h % 2, j * blk:(j + 1) * blk, :] = s
            return jnp.max(s.reshape(blk // 8, 8, qcols), axis=0)

        tops = [None] * heads
        tops[0] = functools.reduce(jnp.maximum, [score(0, j) for j in range(num_blocks)])
        for h in range(heads):
            top = jnp.max(tops[h], axis=0, keepdims=True)
            shift = top * coef
            total, nxt = None, []
            for j in range(num_blocks):
                if h + 1 < heads:
                    nxt.append(score(h + 1, j))
                p = jnp.exp2(scores[h % 2, j * blk:(j + 1) * blk, :] * coef - shift).astype(BF16)
                o = mm(vbuf[slot, j, h], p)
                total = o if total is None else total + o
            if h + 1 < heads:
                tops[h + 1] = functools.reduce(jnp.maximum, nxt)
            msg[k, i, h * hd:(h + 1) * hd, :] = total[:hd]
            msg[k, i, heads * hd + h:heads * hd + h + 1, :] = top
            msg[k, i, heads * hd + heads + h:heads * hd + heads + h + 1, :] = total[hd:hd + 1]

        which = (n % CHUNK) // 2

        @pl.when(i % 2 != core)
        def _():
            remote(msg.at[k, i], rpart.at[k, which], k, which, partner).start()

    stat = heads * hd

    def scales(parts, h):
        tops = [p[stat + h:stat + h + 1, :] for p in parts]
        top = functools.reduce(jnp.maximum, tops)
        return top, [jnp.exp2((t - top) * coef) for t in tops]

    def merge_chip(k):
        remote(msg.at[k, 0], rpart.at[k, 0], k, 0, partner).wait_recv()
        parts = [msg.at[k, 2 * (1 - chip) + core], rpart.at[k, 0]]
        for h in range(heads):
            top, fac = scales(parts, h)
            rows = slice(h * hd, (h + 1) * hd)
            xsend[k, rows, :] = sum(p[rows, :] * f for p, f in zip(parts, fac))
            xsend[k, stat + h:stat + h + 1, :] = top
            srow = slice(stat + heads + h, stat + heads + h + 1)
            xsend[k, srow, :] = sum(p[srow, :] * f for p, f in zip(parts, fac))
        remote(xsend.at[k], xrecv.at[k], k, 2, across_x).start()

    def project(k):
        remote(msg.at[k, 0], rpart.at[k, 1], k, 1, partner).wait_recv()
        remote(xsend.at[k], xrecv.at[k], k, 2, across_x).wait_recv()
        parts = [msg.at[k, cp], rpart.at[k, 1], xrecv.at[k]]
        outs = []
        for h in range(heads):
            _, fac = scales(parts, h)
            rows = slice(h * hd, (h + 1) * hd)
            srow = slice(stat + heads + h, stat + heads + h + 1)
            inv = 1.0 / sum(p[srow, :] * f for p, f in zip(parts, fac))
            outs.append(sum(p[rows, :] * (f * inv) for p, f in zip(parts, fac)))
        attn = jnp.concatenate(outs, axis=0).T.astype(BF16)

        def part(cols):
            acc = None
            for g in range(group):
                d = mm(attn[g * tree:(g + 1) * tree], wout[g, :, cols])
                acc = d if acc is None else acc + d
            return acc.astype(BF16).astype(F32)

        psend[k] = part(other_cols)
        remote(psend.at[k], precv.at[k], k, 3, across_y).start()
        y_ref[k * CHUNK + cp, :, own_cols] = resid[k].astype(F32) + part(own_cols)

    def piece(k, owner_cp, owner_tp, lo=0, n=None):
        rows = pl.ds(lo, tree if n is None else n)
        return y_ref.at[k * CHUNK + owner_cp, rows, pl.ds(pl.multiple_of(owner_tp * wcols, wcols), wcols)]

    hf = tree // 2
    pcp, xcp, dcp = chip * 2 + 1 - core, (1 - chip) * 2 + core, (1 - chip) * 2 + 1 - core

    def gather_copy(k, n):
        if n == 4:
            return remote(piece(k, cp, tp), piece(k, cp, tp), k, n, across_x)
        if n == 5:
            return remote(piece(k, cp, tp), piece(k, cp, tp), k, n, across_y)
        if n == 6:
            return remote(piece(k, cp, tp), piece(k, cp, tp), k, n, partner)
        if n == 7:
            return remote(piece(k, xcp, tp, 0, hf), piece(k, xcp, tp, 0, hf), k, n, across_y)
        if n == 8:
            return remote(piece(k, xcp, tp), piece(k, xcp, tp), k, n, partner)
        if n == 9:
            return remote(piece(k, cp, 1 - tp, hf, hf), piece(k, cp, 1 - tp, hf, hf), k, n, across_x)
        if n == 10:
            return remote(piece(k, cp, 1 - tp), piece(k, cp, 1 - tp), k, n, partner)
        if n == 11:
            return remote(piece(k, xcp, 1 - tp, 0, hf), piece(k, xcp, 1 - tp, 0, hf), k, n, partner)
        return remote(piece(k, xcp, 1 - tp, hf, hf), piece(k, xcp, 1 - tp, hf, hf), k, n, partner)

    def landed(k, n):
        src = {4: (xcp, tp, 0, tree), 5: (cp, 1 - tp, 0, tree), 6: (pcp, tp, 0, tree), 7: (xcp, 1 - tp, 0, hf), 8: (dcp, tp, 0, tree),
               9: (xcp, 1 - tp, hf, hf), 10: (pcp, 1 - tp, 0, tree), 11: (dcp, 1 - tp, 0, hf), 12: (dcp, 1 - tp, hf, hf)}[n]
        ref = piece(k, *src)
        remote(ref, ref, k, n, partner).wait_recv()

    def finish(k):
        remote(psend.at[k], precv.at[k], k, 3, across_y).wait_recv()
        total = y_ref[k * CHUNK + cp, :, own_cols] + precv[k]
        y_ref[k * CHUNK + cp, :, own_cols] = total.astype(BF16).astype(F32)
        for n in (4, 5, 6):
            gather_copy(k, n).start()

    def forward(k):
        landed(k, 4)
        gather_copy(k, 7).start()
        gather_copy(k, 8).start()
        landed(k, 5)
        gather_copy(k, 9).start()
        gather_copy(k, 10).start()

    def forward_diagonal(k):
        landed(k, 7)
        gather_copy(k, 11).start()
        landed(k, 9)
        gather_copy(k, 12).start()

    @pl.loop(0, chunks + 4)
    def _(k):
        @pl.when(k < chunks)
        def _():
            @pl.loop(0, CHUNK)
            def _(ii):
                attend(k * CHUNK + ii)

            merge_chip(k)

        @pl.when((k >= 1) & (k < chunks + 1))
        def _():
            project(k - 1)

        @pl.when((k >= 2) & (k < chunks + 2))
        def _():
            finish(k - 2)

        @pl.when((k >= 3) & (k < chunks + 3))
        def _():
            forward(k - 3)

        @pl.when(k >= 4)
        def _():
            forward_diagonal(k - 4)

    @pl.loop(0, chunks)
    def _(k):
        for n in (6, 8, 10, 11, 12):
            landed(k, n)
        remote(msg.at[k, 0], rpart.at[k, 0], k, 0, partner).wait_send()
        remote(msg.at[k, 0], rpart.at[k, 1], k, 1, partner).wait_send()
        remote(xsend.at[k], xrecv.at[k], k, 2, across_x).wait_send()
        remote(psend.at[k], precv.at[k], k, 3, across_y).wait_send()
        for n in range(4, 13):
            gather_copy(k, n).wait_send()


def solution(mesh):
    cache_spec = P('dp', None, 'cp', 'tp')
    row_spec = P('dp')

    def local_step(hidden, attn_gain, w_query, w_key, w_value, w_out, cache_k, cache_v, ctx_len, positions, tree_mask):
        nreq, tree, width = hidden.shape
        num_blocks, kv_heads, blk, hd = cache_k.shape[1], cache_k.shape[3], cache_k.shape[4], cache_k.shape[5]
        qdim, kvdim = w_query.shape[1], w_key.shape[1]
        group = qdim // kvdim
        chunks = nreq // CHUNK
        rows = CHUNK * tree
        keys = jnp.swapaxes(cache_k[:, :, 0], -1, -2)
        values = jnp.swapaxes(cache_v[:, :, 0], -1, -2)
        cos, sin = rope_tables(positions.reshape(chunks, rows), hd)
        hbm = pl.BlockSpec(memory_space=pl.ANY)
        vmem = pl.BlockSpec(memory_space=pltpu.VMEM)
        smem = pl.BlockSpec(memory_space=pltpu.SMEM)
        cache_shape = jax.ShapeDtypeStruct(keys.shape, BF16)
        query, new_keys, new_vals = pl.pallas_call(
            qkv_kernel,
            grid=(chunks,),
            in_specs=[smem, pl.BlockSpec((rows, width), lambda s: (s, 0)), pl.BlockSpec((1, width), lambda s: (0, 0)),
                      pl.BlockSpec((width, qdim), lambda s: (0, 0)), pl.BlockSpec((width, kvdim), lambda s: (0, 0)), pl.BlockSpec((width, kvdim), lambda s: (0, 0)),
                      pl.BlockSpec((1, hd // 2, rows), lambda s: (s, 0, 0)), pl.BlockSpec((1, hd // 2, rows), lambda s: (s, 0, 0)), hbm, hbm],
            out_specs=[pl.BlockSpec((CHUNK, kv_heads, hd, group * tree), lambda s: (s, 0, 0, 0)), hbm, hbm],
            out_shape=[jax.ShapeDtypeStruct((nreq, kv_heads, hd, group * tree), BF16), cache_shape, cache_shape],
            scratch_shapes=[pltpu.VMEM((2, 2, CHUNK, num_blocks, kv_heads, hd, blk), BF16), pltpu.VMEM((2, kvdim, rows), BF16),
                            pltpu.SemaphoreType.DMA((2, 2)), pltpu.SemaphoreType.DMA((2, 2))],
            compiler_params=pltpu.CompilerParams(vmem_limit_bytes=58 * 2**20),
            name='qkv_and_cache',
        )(ctx_len, hidden.reshape(nreq * tree, width), attn_gain.reshape(1, width), w_query, w_key, w_value, cos, sin, keys, values)
        bias = jnp.where(jnp.swapaxes(tree_mask, 1, 2) > 0, 0.0, MASKED).astype(BF16)
        bias = jnp.tile(bias, (1, 1, group))
        qcols = group * tree
        rows_msg = kv_heads * hd + 2 * kv_heads
        ext = hd + tree + 16
        wide_y = pl.pallas_call(
            attend_kernel,
            in_specs=[smem, vmem, vmem, hbm, hbm, hbm, hbm],
            out_specs=vmem,
            out_shape=jax.ShapeDtypeStruct((nreq, tree, width), F32),
            scratch_shapes=[
                pltpu.VMEM((2, num_blocks, kv_heads, hd, blk), BF16),
                pltpu.VMEM((2, num_blocks, kv_heads, hd + 16, blk), BF16),
                pltpu.VMEM((num_blocks - num_blocks // 2, kv_heads, ext, blk), BF16),
                pltpu.VMEM((kv_heads, ext, qcols), BF16),
                pltpu.VMEM((2, num_blocks * blk, qcols), F32),
                pltpu.VMEM((chunks, CHUNK, rows_msg, qcols), F32),
                pltpu.VMEM((chunks, 2, rows_msg, qcols), F32),
                pltpu.VMEM((chunks, rows_msg, qcols), F32),
                pltpu.VMEM((chunks, rows_msg, qcols), F32),
                pltpu.VMEM((chunks, tree, width // 2), F32),
                pltpu.VMEM((chunks, tree, width // 2), F32),
                pltpu.VMEM((group, kv_heads * hd, width), BF16),
                pltpu.VMEM((chunks, tree, width // 2), BF16),
                pltpu.SemaphoreType.DMA((2, 2)),
                pltpu.SemaphoreType.DMA((group, kv_heads)),
                pltpu.SemaphoreType.DMA((chunks,)),
                pltpu.SemaphoreType.DMA((chunks, 13)),
                pltpu.SemaphoreType.DMA((chunks, 13)),
            ],
            compiler_params=pltpu.CompilerParams(collective_id=0, has_side_effects=True, vmem_limit_bytes=62 * 2**20),
            name='attend_and_combine',
        )(ctx_len, query, bias, new_keys, new_vals, hidden, w_out)
        return (wide_y.astype(BF16), jnp.swapaxes(new_keys, -1, -2)[:, :, None], jnp.swapaxes(new_vals, -1, -2)[:, :, None])

    return jax.shard_map(local_step, mesh=mesh, in_specs=(row_spec, P(), P(None, 'tp'), P(None, 'tp'), P(None, 'tp'), P('tp', None), cache_spec, cache_spec, row_spec, row_spec, row_spec), out_specs=(row_spec, cache_spec, cache_spec), check_vma=False)
```

profile of v0, /device:TPU:0, one launch (start us, length us, event | category | flops | bytes accessed | tf_op | source)
XLA Modules:
  0.0 163.0 jit_solution(5090711643001586632)
XLA Ops:
  0.7 1.3 reshape.46.gain_ref
  1.9 0.7 convert_element_type.19
  2.7 0.1 convert_element_type.20
  2.7 1.5 multiply_sine_fusion
  4.2 1.2 fusion
  5.5 0.2 copy.14
  5.7 0.6 tile.4
  6.3 1.8 %tile.10.bias_ref = bf16[24,64,256]{2,1,0:T(8,128)(2,1)} reshape(bf16[24,64,4,64]{3,2,1,0:T(4,128)(2,1)S(1)} %tile.4) | data formatting | bytes 1572864 | tf_op jit(solution)/shard_map/tile | solution.py:412
  8.0 25.6 %qkv_and_cache.1 = (bf16[24,4,64,256]{3,2,1,0:T(8,128)(2,1)}, bf16[24,4,4,64,256]{4,3,2,1,0:T(8,128)(2,1)}, bf16[24,4,4,64,256]{4,3,2,1,0:T(8,128)(2,1)}) custom-call(s32[24]{0:T(128)} %ctx_ref.3, bf16[1536,2048]{1,0:T(8,128)(2,1)} %bitcast.19, bf16[1,2048]{1,0:T(2,128)(2,1)} %reshape.46.gain_ref, bf16[2048,1024]{1,0:T(8,128)(2,1)} %wq_ref.1, ...), custom_call_target="tpu_custom_call" | custom-call | tf_op jit(solution)/shard_map/qkv_and_cache/pallas_call | solution.py:398
  33.7 121.1 %attend_and_combine.1 = f32[24,64,2048]{2,1,0:T(8,128)} custom-call(s32[24]{0:T(128)} %ctx_ref.3, bf16[24,4,64,256]{3,2,1,0:T(8,128)(2,1)} %get-tuple-element.6.q_ref, bf16[24,64,256]{2,1,0:T(8,128)(2,1)} %tile.10.bias_ref, bf16[24,4,4,64,256]{4,3,2,1,0:T(8,128)(2,1)} %get-tuple-element.7.kc_hbm, bf16[24,4,4,64,256]{4,3,2,1,0:T(8,128)(2,1)} %get-tuple-element.8.vc_hbm, ...), custom_call_target="tpu_custom_call" | custom-call | tf_op jit(solution)/shard_map/attend_and_combine/pallas_call | solution.py:416
  154.8 8.3 %convert_element_type.23 = bf16[24,64,2048]{2,1,0:T(8,128)(2,1)} convert(f32[24,64,2048]{2,1,0:T(8,128)} %attend_and_combine.1) | non-fusion elementwise | flops 3145728 | bytes 18874368 | tf_op jit(solution)/shard_map/convert_element_type | solution.py:444
  (1 shorter events, 0.0 us)
where the time goes:
time: 163 us
  Pallas kernels  147 us (90%)
  other arithmetic  11.7 us (7%)
  local copies, waits for them, and re-layouts  3.92 us (2%)
    pallas_call x1, Pallas kernels, local_step(): pl.pallas_call(attend_kernel, in_specs=[smem, vmem, vmem, hbm, hbm, hbm,...  121 us
    pallas_call x1, Pallas kernels, local_step(): pl.pallas_call(qkv_kernel, grid=(chunks,), in_specs=[smem, pl.BlockSpec((...  25.6 us
    convert_element_type x1, other arithmetic, local_step(): wide_y.astype(BF16)  8.27 us

commit v1 on v0

--- a/solution.py
+++ b/solution.py
@@ -2,6 +2,7 @@
 import math
 import jax
 import jax.numpy as jnp
+import numpy as np
 from jax import lax
 from jax.experimental import pallas as pl
 from jax.experimental.pallas import tpu as pltpu
@@ -25,18 +26,17 @@
     return lax.dot_general(a, b, (((0,), (0,)), ((), ())), preferred_element_type=F32)
 
 
-def rope_tables(positions, head_dim):
-    freq_idx = jnp.arange(head_dim // 2, dtype=F32)
-    inv_freq = 1.0 / (ROPE_THETA ** (2.0 * freq_idx / head_dim))
-    wavelen = 2.0 * math.pi / inv_freq
-    smooth = (8192.0 / wavelen - 1.0) / 3.0
-    blended = (1.0 - smooth) * inv_freq / 8.0 + smooth * inv_freq
-    inv_freq = jnp.where(wavelen < 2048.0, inv_freq, jnp.where(wavelen > 8192.0, inv_freq / 8.0, blended))
-    angle = positions.astype(F32)[:, None, :] * inv_freq[None, :, None]
-    return jnp.cos(angle), jnp.sin(angle)
-
-
-def qkv_kernel(ctx_ref, x_ref, gain_ref, wq_ref, wk_ref, wv_ref, cos_ref, sin_ref, kc_hbm, vc_hbm,
+def rope_frequencies(head_dim):
+    freq_idx = np.arange(head_dim // 2, dtype=np.float32)
+    inv_freq = np.float32(1.0) / (np.float32(ROPE_THETA) ** (np.float32(2.0) * freq_idx / np.float32(head_dim)))
+    wavelen = np.float32(2.0 * math.pi) / inv_freq
+    smooth = (np.float32(8192.0) / wavelen - np.float32(1.0)) / np.float32(3.0)
+    blended = (np.float32(1.0) - smooth) * inv_freq / np.float32(8.0) + smooth * inv_freq
+    inv_freq = np.where(wavelen < 2048.0, inv_freq, np.where(wavelen > 8192.0, inv_freq / np.float32(8.0), blended))
+    return np.broadcast_to(inv_freq.astype(np.float32)[:, None], (head_dim // 2, 128))
+
+
+def qkv_kernel(ctx_ref, x_ref, gain_ref, wq_ref, wk_ref, wv_ref, pos_ref, freq_ref, kc_hbm, vc_hbm,
                q_ref, ko_hbm, vo_hbm, buf, new_ref, in_sem, out_sem):
     step, steps = pl.program_id(0), pl.num_programs(0)
     cp_rank, cp_size = lax.axis_index('cp'), lax.axis_size('cp')
@@ -72,8 +72,10 @@
 
     wide = x_ref[...].astype(F32)
     inv_rms = lax.rsqrt(jnp.mean(wide * wide, axis=-1, keepdims=True) + NORM_EPS)
-    h = (wide * inv_rms * gain_ref[...].astype(F32)).astype(BF16)
-    cos, sin = cos_ref[0], sin_ref[0]
+    h = (wide * inv_rms * gain_ref[...].astype(F32)[None, :]).astype(BF16)
+    pos = jnp.concatenate([pos_ref[pl.ds(step * CHUNK + i, 1), :] for i in range(CHUNK)], axis=1).astype(F32)
+    angle = pos * freq_ref[:, 0:1]
+    cos, sin = jnp.cos(angle), jnp.sin(angle)
 
     def rotate(rows):
         first, second = rows[:half], rows[half:]
@@ -120,19 +122,18 @@
             c.wait()
 
 
-def attend_kernel(ctx_ref, q_ref, bias_ref, kc_hbm, vc_hbm, hid_hbm, wo_hbm, y_ref,
-                  kbuf, vbuf, kext, qext, scores, msg, rpart, xsend, xrecv, psend, precv, wout, resid,
-                  kv_sem, w_sem, hid_sem, snd, rcv):
+def attend_kernel(ctx_ref, q_hbm, mask_hbm, kc_hbm, vc_hbm, hid_hbm, wo_hbm, out_hbm,
+                  y_ref, kbuf, vbuf, kext, qext, mbuf, scores, msg, rpart, xsend, xrecv, psend, precv, wout, resid, stage,
+                  kv_sem, w_sem, hid_sem, out_sem, snd, rcv):
     cp, tp = lax.axis_index('cp'), lax.axis_index('tp')
     chip, core = cp // 2, cp % 2
     partner = {'cp': chip * 2 + 1 - core}
     across_x = {'cp': (1 - chip) * 2 + core}
     across_y = {'tp': 1 - tp}
-    heads, hd, qcols = q_ref.shape[1:]
-    tree = bias_ref.shape[1]
+    nreq, heads, hd, qcols = q_hbm.shape
+    tree = mask_hbm.shape[1]
     group = qcols // tree
     num_blocks, blk = kbuf.shape[1], kbuf.shape[4]
-    nreq = q_ref.shape[0]
     chunks = nreq // CHUNK
     width = wo_hbm.shape[1]
     wcols = width // 2
@@ -153,7 +154,9 @@
     def fetch(n):
         r, to = request_of(n), n % 2
         return [pltpu.make_async_copy(kc_hbm.at[r], kbuf.at[to], kv_sem.at[to, 0]),
-                pltpu.make_async_copy(vc_hbm.at[r], vbuf.at[to, :, :, pl.ds(0, hd), :], kv_sem.at[to, 1])]
+                pltpu.make_async_copy(vc_hbm.at[r], vbuf.at[to, :, :, pl.ds(0, hd), :], kv_sem.at[to, 1]),
+                pltpu.make_async_copy(q_hbm.at[r], qext.at[to, :, pl.ds(0, hd), :], kv_sem.at[to, 2]),
+                pltpu.make_async_copy(mask_hbm.at[r], mbuf.at[to], kv_sem.at[to, 3])]
 
     def weight_copies():
         out = []
@@ -174,13 +177,12 @@
         for j in range(num_blocks):
             for h in range(heads):
                 vbuf[s, j, h, hd:, :] = ones
-    pad = qext.shape[1] - hd - tree
+    pad = qext.shape[2] - hd - tree
     hide = jnp.where(lax.broadcasted_iota(jnp.int32, (pad, qcols), 0) == 0, MASKED, 0.0).astype(BF16)
-    for h in range(heads):
-        qext[h, hd + tree:, :] = hide
+    for s in range(2):
+        for h in range(heads):
+            qext[s, h, hd + tree:, :] = hide
     pl.semaphore_wait(barrier, 3)
-    for c in weight_copies() + resid_copies():
-        c.wait()
 
     def attend(n):
         k, r, slot = n // CHUNK, request_of(n), n % 2
@@ -192,12 +194,12 @@
                 c.start()
 
         ctx = ctx_ref[r]
-        bias = bias_ref[r]
-        for h in range(heads):
-            qext[h, :hd, :] = q_ref[r, h]
-            qext[h, hd:hd + tree, :] = bias
         for c in fetch(n):
             c.wait()
+        seen = jnp.concatenate([mbuf[slot].astype(F32)] * group, axis=0).T
+        bias = jnp.where(seen > 0.0, 0.0, MASKED).astype(BF16)
+        for h in range(heads):
+            qext[slot, h, hd:hd + tree, :] = bias
         late = num_blocks // 2
         for j in range(late, num_blocks):
             off = (j * 4 + cp) * blk - ctx
@@ -213,9 +215,9 @@
 
         def score(h, j):
             if j < late:
-                s = mm_tn(kbuf[slot, j, h], qext[h, :hd, :])
+                s = mm_tn(kbuf[slot, j, h], qext[slot, h, :hd, :])
             else:
-                s = mm_tn(kext[j - late, h], qext[h])
+                s = mm_tn(kext[j - late, h], qext[slot, h])
             scores[h % 2, j * blk:(j + 1) * blk, :] = s
             return jnp.max(s.reshape(blk // 8, 8, qcols), axis=0)
 
@@ -275,6 +277,11 @@
             outs.append(sum(p[rows, :] * (f * inv) for p, f in zip(parts, fac)))
         attn = jnp.concatenate(outs, axis=0).T.astype(BF16)
 
+        @pl.when(k == 0)
+        def _():
+            for c in weight_copies() + resid_copies():
+                c.wait()
+
         def part(cols):
             acc = None
             for g in range(group):
@@ -290,7 +297,8 @@
         rows = pl.ds(lo, tree if n is None else n)
         return y_ref.at[k * CHUNK + owner_cp, rows, pl.ds(pl.multiple_of(owner_tp * wcols, wcols), wcols)]
 
-    hf = tree // 2
+    hf = (tree * 3 // 8) // 8 * 8
+    hb = tree - hf
     pcp, xcp, dcp = chip * 2 + 1 - core, (1 - chip) * 2 + core, (1 - chip) * 2 + 1 - core
 
     def gather_copy(k, n):
@@ -305,16 +313,16 @@
         if n == 8:
             return remote(piece(k, xcp, tp), piece(k, xcp, tp), k, n, partner)
         if n == 9:
-            return remote(piece(k, cp, 1 - tp, hf, hf), piece(k, cp, 1 - tp, hf, hf), k, n, across_x)
+            return remote(piece(k, cp, 1 - tp, hf, hb), piece(k, cp, 1 - tp, hf, hb), k, n, across_x)
         if n == 10:
             return remote(piece(k, cp, 1 - tp), piece(k, cp, 1 - tp), k, n, partner)
         if n == 11:
             return remote(piece(k, xcp, 1 - tp, 0, hf), piece(k, xcp, 1 - tp, 0, hf), k, n, partner)
-        return remote(piece(k, xcp, 1 - tp, hf, hf), piece(k, xcp, 1 - tp, hf, hf), k, n, partner)
+        return remote(piece(k, xcp, 1 - tp, hf, hb), piece(k, xcp, 1 - tp, hf, hb), k, n, partner)
 
     def landed(k, n):
         src = {4: (xcp, tp, 0, tree), 5: (cp, 1 - tp, 0, tree), 6: (pcp, tp, 0, tree), 7: (xcp, 1 - tp, 0, hf), 8: (dcp, tp, 0, tree),
-               9: (xcp, 1 - tp, hf, hf), 10: (pcp, 1 - tp, 0, tree), 11: (dcp, 1 - tp, 0, hf), 12: (dcp, 1 - tp, hf, hf)}[n]
+               9: (xcp, 1 - tp, hf, hb), 10: (pcp, 1 - tp, 0, tree), 11: (dcp, 1 - tp, 0, hf), 12: (dcp, 1 - tp, hf, hb)}[n]
         ref = piece(k, *src)
         remote(ref, ref, k, n, partner).wait_recv()
 
@@ -339,36 +347,41 @@
         landed(k, 9)
         gather_copy(k, 12).start()
 
-    @pl.loop(0, chunks + 4)
-    def _(k):
-        @pl.when(k < chunks)
+    def out_copy(k):
+        return pltpu.make_async_copy(stage.at[k % 2], out_hbm.at[pl.ds(k * CHUNK, CHUNK)], out_sem.at[k % 2])
+
+    def emit(k):
+        for n in (6, 8, 10, 11, 12):
+            landed(k, n)
+
+        @pl.when(k >= 2)
         def _():
-            @pl.loop(0, CHUNK)
-            def _(ii):
-                attend(k * CHUNK + ii)
-
-            merge_chip(k)
-
-        @pl.when((k >= 1) & (k < chunks + 1))
+            out_copy(k - 2).wait()
+
+        for i in range(CHUNK):
+            stage[k % 2, i] = y_ref[k * CHUNK + i].astype(BF16)
+        out_copy(k).start()
+
+    steps = ((merge_chip, 3), (project, 7), (finish, 11), (forward, 15), (forward_diagonal, 19), (emit, 23))
+
+    @pl.loop(0, nreq + steps[-1][1])
+    def _(n):
+        @pl.when(n < nreq)
         def _():
-            project(k - 1)
-
-        @pl.when((k >= 2) & (k < chunks + 2))
-        def _():
-            finish(k - 2)
-
-        @pl.when((k >= 3) & (k < chunks + 3))
-        def _():
-            forward(k - 3)
-
-        @pl.when(k >= 4)
-        def _():
-            forward_diagonal(k - 4)
+            attend(n)
+
+        for work, after in steps:
+            since = n + 1 - after
+
+            @pl.when((since >= 0) & (since < nreq) & (since % CHUNK == 0))
+            def _():
+                work(since // CHUNK)
+
+    for k in range(chunks - 2, chunks):
+        out_copy(k).wait()
 
     @pl.loop(0, chunks)
     def _(k):
-        for n in (6, 8, 10, 11, 12):
-            landed(k, n)
         remote(msg.at[k, 0], rpart.at[k, 0], k, 0, partner).wait_send()
         remote(msg.at[k, 0], rpart.at[k, 1], k, 1, partner).wait_send()
         remote(xsend.at[k], xrecv.at[k], k, 2, across_x).wait_send()
@@ -390,39 +403,37 @@
         rows = CHUNK * tree
         keys = jnp.swapaxes(cache_k[:, :, 0], -1, -2)
         values = jnp.swapaxes(cache_v[:, :, 0], -1, -2)
-        cos, sin = rope_tables(positions.reshape(chunks, rows), hd)
         hbm = pl.BlockSpec(memory_space=pl.ANY)
-        vmem = pl.BlockSpec(memory_space=pltpu.VMEM)
         smem = pl.BlockSpec(memory_space=pltpu.SMEM)
         cache_shape = jax.ShapeDtypeStruct(keys.shape, BF16)
         query, new_keys, new_vals = pl.pallas_call(
             qkv_kernel,
             grid=(chunks,),
-            in_specs=[smem, pl.BlockSpec((rows, width), lambda s: (s, 0)), pl.BlockSpec((1, width), lambda s: (0, 0)),
+            in_specs=[smem, pl.BlockSpec((rows, width), lambda s: (s, 0)), pl.BlockSpec((width,), lambda s: (0,)),
                       pl.BlockSpec((width, qdim), lambda s: (0, 0)), pl.BlockSpec((width, kvdim), lambda s: (0, 0)), pl.BlockSpec((width, kvdim), lambda s: (0, 0)),
-                      pl.BlockSpec((1, hd // 2, rows), lambda s: (s, 0, 0)), pl.BlockSpec((1, hd // 2, rows), lambda s: (s, 0, 0)), hbm, hbm],
+                      pl.BlockSpec((nreq, tree), lambda s: (0, 0)), pl.BlockSpec((hd // 2, 128), lambda s: (0, 0)), hbm, hbm],
             out_specs=[pl.BlockSpec((CHUNK, kv_heads, hd, group * tree), lambda s: (s, 0, 0, 0)), hbm, hbm],
             out_shape=[jax.ShapeDtypeStruct((nreq, kv_heads, hd, group * tree), BF16), cache_shape, cache_shape],
             scratch_shapes=[pltpu.VMEM((2, 2, CHUNK, num_blocks, kv_heads, hd, blk), BF16), pltpu.VMEM((2, kvdim, rows), BF16),
                             pltpu.SemaphoreType.DMA((2, 2)), pltpu.SemaphoreType.DMA((2, 2))],
             compiler_params=pltpu.CompilerParams(vmem_limit_bytes=58 * 2**20),
             name='qkv_and_cache',
-        )(ctx_len, hidden.reshape(nreq * tree, width), attn_gain.reshape(1, width), w_query, w_key, w_value, cos, sin, keys, values)
-        bias = jnp.where(jnp.swapaxes(tree_mask, 1, 2) > 0, 0.0, MASKED).astype(BF16)
-        bias = jnp.tile(bias, (1, 1, group))
+        )(ctx_len, hidden.reshape(nreq * tree, width), attn_gain, w_query, w_key, w_value, positions, jnp.asarray(rope_frequencies(hd)), keys, values)
         qcols = group * tree
         rows_msg = kv_heads * hd + 2 * kv_heads
         ext = hd + tree + 16
-        wide_y = pl.pallas_call(
+        out_hidden = pl.pallas_call(
             attend_kernel,
-            in_specs=[smem, vmem, vmem, hbm, hbm, hbm, hbm],
-            out_specs=vmem,
-            out_shape=jax.ShapeDtypeStruct((nreq, tree, width), F32),
+            in_specs=[smem, hbm, hbm, hbm, hbm, hbm, hbm],
+            out_specs=hbm,
+            out_shape=jax.ShapeDtypeStruct((nreq, tree, width), BF16),
             scratch_shapes=[
+                pltpu.VMEM((nreq, tree, width), F32),
                 pltpu.VMEM((2, num_blocks, kv_heads, hd, blk), BF16),
                 pltpu.VMEM((2, num_blocks, kv_heads, hd + 16, blk), BF16),
                 pltpu.VMEM((num_blocks - num_blocks // 2, kv_heads, ext, blk), BF16),
-                pltpu.VMEM((kv_heads, ext, qcols), BF16),
+                pltpu.VMEM((2, kv_heads, ext, qcols), BF16),
+                pltpu.VMEM((2, tree, tree), jnp.int32),
                 pltpu.VMEM((2, num_blocks * blk, qcols), F32),
                 pltpu.VMEM((chunks, CHUNK, rows_msg, qcols), F32),
                 pltpu.VMEM((chunks, 2, rows_msg, qcols), F32),
@@ -432,15 +443,17 @@
                 pltpu.VMEM((chunks, tree, width // 2), F32),
                 pltpu.VMEM((group, kv_heads * hd, width), BF16),
                 pltpu.VMEM((chunks, tree, width // 2), BF16),
-                pltpu.SemaphoreType.DMA((2, 2)),
+                pltpu.VMEM((2, CHUNK, tree, width), BF16),
+                pltpu.SemaphoreType.DMA((2, 4)),
                 pltpu.SemaphoreType.DMA((group, kv_heads)),
                 pltpu.SemaphoreType.DMA((chunks,)),
+                pltpu.SemaphoreType.DMA((2,)),
                 pltpu.SemaphoreType.DMA((chunks, 13)),
                 pltpu.SemaphoreType.DMA((chunks, 13)),
             ],
             compiler_params=pltpu.CompilerParams(collective_id=0, has_side_effects=True, vmem_limit_bytes=62 * 2**20),
             name='attend_and_combine',
-        )(ctx_len, query, bias, new_keys, new_vals, hidden, w_out)
-        return (wide_y.astype(BF16), jnp.swapaxes(new_keys, -1, -2)[:, :, None], jnp.swapaxes(new_vals, -1, -2)[:, :, None])
+        )(ctx_len, query, tree_mask, new_keys, new_vals, hidden, w_out)
+        return (out_hidden, jnp.swapaxes(new_keys, -1, -2)[:, :, None], jnp.swapaxes(new_vals, -1, -2)[:, :, None])
 
     return jax.shard_map(local_step, mesh=mesh, in_specs=(row_spec, P(), P(None, 'tp'), P(None, 'tp'), P(None, 'tp'), P('tp', None), cache_spec, cache_spec, row_spec, row_spec, row_spec), out_specs=(row_spec, cache_spec, cache_spec), check_vma=False)

time: 163 us -> 153 us (0.939)
  other arithmetic: 11.7 us -> 0 us
  local copies, waits for them, and re-layouts: 3.92 us -> 7.94 us
  Pallas kernels: 147 us -> 144 us
    convert_element_type x3 -> x0, other arithmetic: 10.2 us -> none  [the longest x1 8.27 us: local_step(): wide_y.astype(BF16)]
    unnamed x0 -> x1, local copies, waits for them, and re-layouts: none -> 6.61 us
    pallas_call x1, Pallas kernels: 121 us -> 115 us  [local_step(): pl.pallas_call(attend_kernel, in_specs=[smem, hbm, hbm, hbm, hbm, hbm, hb...]
    pallas_call x1, Pallas kernels: 25.6 us -> 29.5 us  [local_step(): pl.pallas_call(qkv_kernel, grid=(chunks,), in_specs=[smem, pl.BlockSpec((...]
where the time goes in v1:
time: 153 us
  Pallas kernels  144 us (94%)
  local copies, waits for them, and re-layouts  7.94 us (5%)
    pallas_call x1, Pallas kernels, local_step(): pl.pallas_call(attend_kernel, in_specs=[smem, hbm, hbm, hbm, hbm, hbm, hb...  115 us
    pallas_call x1, Pallas kernels, local_step(): pl.pallas_call(qkv_kernel, grid=(chunks,), in_specs=[smem, pl.BlockSpec((...  29.5 us
    unnamed x1, local copies, waits for them, and re-layouts  6.61 us

profile of v1, /device:TPU:0, one launch (start us, length us, event | category | flops | bytes accessed | tf_op | source)
XLA Modules:
  0.0 152.9 jit_solution(7561700616364307221)
XLA Ops:
  0.6 1.3 jit_solution_.3.freq_ref
  2.0 29.5 %qkv_and_cache.1 = (bf16[24,4,64,256]{3,2,1,0:T(8,128)(2,1)}, bf16[24,4,4,64,256]{4,3,2,1,0:T(8,128)(2,1)}, bf16[24,4,4,64,256]{4,3,2,1,0:T(8,128)(2,1)}) custom-call(s32[24]{0:T(128)} %ctx_ref.3, bf16[1536,2048]{1,0:T(8,128)(2,1)} %bitcast.17, bf16[2048]{0:T(1024)(128)(2,1)} %gain_ref.1, bf16[2048,1024]{1,0:T(8,128)(2,1)} %wq_ref.1, ...), custom_call_target="tpu_custom_call" | custom-call | tf_op jit(solution)/shard_map/qkv_and_cache/pallas_call | solution.py:409
  31.4 114.8 %attend_and_combine.1 = bf16[24,64,2048]{2,1,0:T(8,128)(2,1)} custom-call(s32[24]{0:T(128)} %ctx_ref.3, bf16[24,4,64,256]{3,2,1,0:T(8,128)(2,1)} %get-tuple-element.6.q_hbm, s32[24,64,64]{2,1,0:T(8,128)} %mask_hbm.1, bf16[24,4,4,64,256]{4,3,2,1,0:T(8,128)(2,1)} %get-tuple-element.7.kc_hbm, bf16[24,4,4,64,256]{4,3,2,1,0:T(8,128)(2,1)} %get-tuple-element.8.vc_hbm, ...), custom_call_target="tpu_custom_call" | custom-call | tf_op jit(solution)/shard_map/attend_and_combine/pallas_call | solution.py:425
  146.2 6.6 %copy.18 = bf16[24,64,2048]{2,1,0:T(8,128)(2,1)} copy(bf16[24,64,2048]{2,1,0:T(8,128)(2,1)} %attend_and_combine.1) | data formatting | bytes 12582912

commit v2 on v1

--- a/solution.py
+++ b/solution.py
@@ -32,65 +32,88 @@
     wavelen = np.float32(2.0 * math.pi) / inv_freq
     smooth = (np.float32(8192.0) / wavelen - np.float32(1.0)) / np.float32(3.0)
     blended = (np.float32(1.0) - smooth) * inv_freq / np.float32(8.0) + smooth * inv_freq
-    inv_freq = np.where(wavelen < 2048.0, inv_freq, np.where(wavelen > 8192.0, inv_freq / np.float32(8.0), blended))
-    return np.broadcast_to(inv_freq.astype(np.float32)[:, None], (head_dim // 2, 128))
-
-
-def qkv_kernel(ctx_ref, x_ref, gain_ref, wq_ref, wk_ref, wv_ref, pos_ref, freq_ref, kc_hbm, vc_hbm,
-               q_ref, ko_hbm, vo_hbm, buf, new_ref, in_sem, out_sem):
+    return np.where(wavelen < 2048.0, inv_freq, np.where(wavelen > 8192.0, inv_freq / np.float32(8.0), blended)).astype(np.float32)
+
+
+def normed_rows(x, gain):
+    wide = x.astype(F32)
+    inv_rms = lax.rsqrt(jnp.mean(wide * wide, axis=-1, keepdims=True) + NORM_EPS)
+    return (wide * inv_rms * gain.astype(F32)[None, :]).astype(BF16)
+
+
+def rotate(rows, cos, sin):
+    half = rows.shape[0] // 2
+    first, second = rows[:half], rows[half:]
+    return jnp.concatenate([first * cos - second * sin, second * cos + first * sin], axis=0)
+
+
+def project_queries(h, wq_ref, cos, sin, out, hd, group, tree):
+    reqs = h.shape[0] // tree
+    for head in range(wq_ref.shape[1] // (group * hd)):
+        q_t = mm(h, wq_ref[:, head * group * hd:(head + 1) * group * hd]).T
+        parts = [rotate(q_t[g * hd:(g + 1) * hd], cos, sin) for g in range(group)]
+        for i in range(reqs):
+            out(i, head, jnp.concatenate([p[:, i * tree:(i + 1) * tree] for p in parts], axis=1).astype(BF16))
+
+
+def cache_kernel(ctx_ref, x_ref, gain_ref, wk_ref, wv_ref, pos_ref, freq_ref, wq_hbm, kc_hbm, vc_hbm,
+                 q_ref, tab_ref, ko_hbm, vo_hbm, buf, new_ref, wq_ref, in_sem, out_sem, w_sem):
     step, steps = pl.program_id(0), pl.num_programs(0)
     cp_rank, cp_size = lax.axis_index('cp'), lax.axis_size('cp')
-    slot = lax.rem(step, 2)
-    num_blocks, kv_heads, hd, blk = buf.shape[3:]
-    half = hd // 2
-    tree = x_ref.shape[0] // CHUNK
-    heads = q_ref.shape[1]
+    slots, _, per, num_blocks, kv_heads, hd, blk = buf.shape
+    slot = lax.rem(step, slots)
+    tree = pos_ref.shape[1]
     group = q_ref.shape[3] // tree
-
-    def fetch(idx, to):
-        rows = pl.ds(idx * CHUNK, CHUNK)
+    first_req = (steps - 1 - step) * per
+
+    def fetch(idx):
+        rows, to = pl.ds((steps - 1 - idx) * per, per), lax.rem(idx, slots)
         return [pltpu.make_async_copy(src.at[rows], buf.at[to, n], in_sem.at[to, n]) for n, src in enumerate((kc_hbm, vc_hbm))]
 
-    def flush(idx, frm):
-        rows = pl.ds(idx * CHUNK, CHUNK)
+    def flush(idx):
+        rows, frm = pl.ds((steps - 1 - idx) * per, per), lax.rem(idx, slots)
         return [pltpu.make_async_copy(buf.at[frm, n], dst.at[rows], out_sem.at[frm, n]) for n, dst in enumerate((ko_hbm, vo_hbm))]
+
+    wq_copy = pltpu.make_async_copy(wq_hbm, wq_ref, w_sem)
 
     @pl.when(step == 0)
     def _():
-        for c in fetch(0, 0):
+        for c in fetch(0) + fetch(1):
             c.start()
 
-    @pl.when(step >= 1)
+    @pl.when(step == 1)
     def _():
-        for c in flush(step - 1, 1 - slot):
-            c.wait()
-
-    @pl.when(step + 1 < steps)
+        wq_copy.start()
+
+    @pl.when(step + 2 < steps)
     def _():
-        for c in fetch(step + 1, 1 - slot):
+        @pl.when(step + 2 >= slots)
+        def _():
+            for c in flush(step + 2 - slots):
+                c.wait()
+
+        for c in fetch(step + 2):
             c.start()
 
-    wide = x_ref[...].astype(F32)
-    inv_rms = lax.rsqrt(jnp.mean(wide * wide, axis=-1, keepdims=True) + NORM_EPS)
-    h = (wide * inv_rms * gain_ref[...].astype(F32)[None, :]).astype(BF16)
-    pos = jnp.concatenate([pos_ref[pl.ds(step * CHUNK + i, 1), :] for i in range(CHUNK)], axis=1).astype(F32)
-    angle = pos * freq_ref[:, 0:1]
+    h = normed_rows(x_ref[...], gain_ref[...])
+    half = hd // 2
+    diag = lax.broadcasted_iota(jnp.int32, (half, half), 0) == lax.broadcasted_iota(jnp.int32, (half, half), 1)
+    freq = jnp.sum(jnp.where(diag, freq_ref[...][None, :], 0.0), axis=1, keepdims=True)
+    pos = jnp.concatenate([pos_ref[pl.ds(first_req + i, 1), :] for i in range(per)], axis=1).astype(F32)
+    angle = pos * freq
     cos, sin = jnp.cos(angle), jnp.sin(angle)
-
-    def rotate(rows):
-        first, second = rows[:half], rows[half:]
-        return jnp.concatenate([first * cos - second * sin, second * cos + first * sin], axis=0)
-
+    tab_ref[0, 0] = cos
+    tab_ref[0, 1] = sin
     key_t = mm(h, wk_ref[...]).T
     for n in range(kv_heads):
-        new_ref[0, n * hd:(n + 1) * hd, :] = rotate(key_t[n * hd:(n + 1) * hd]).astype(BF16)
+        new_ref[0, n * hd:(n + 1) * hd, :] = rotate(key_t[n * hd:(n + 1) * hd], cos, sin).astype(BF16)
     new_ref[1] = mm(h, wv_ref[...]).T.astype(BF16)
 
-    for c in fetch(step, slot):
+    for c in fetch(step):
         c.wait()
-    cols = CHUNK * tree
-    for i in range(CHUNK):
-        ctx = ctx_ref[step * CHUNK + i]
+    cols = per * tree
+    for i in range(per):
+        ctx = ctx_ref[first_req + i]
         for j in range(num_blocks // 2, num_blocks):
             first_pos = (j * cp_size + cp_rank) * blk
 
@@ -107,30 +130,39 @@
                         old = buf[slot, n, i, j, head].astype(F32)
                         buf[slot, n, i, j, head] = jnp.where(fresh, put[head * hd:(head + 1) * hd], old).astype(BF16)
 
-    for c in flush(step, slot):
+    for c in flush(step):
         c.start()
-    for head in range(heads):
-        cols_h = pl.ds(head * group * hd, group * hd)
-        q_t = mm(h, wq_ref[:, cols_h]).T
-        parts = [rotate(q_t[g * hd:(g + 1) * hd]) for g in range(group)]
-        for i in range(CHUNK):
-            q_ref[i, head] = jnp.concatenate([p[:, i * tree:(i + 1) * tree] for p in parts], axis=1).astype(BF16)
+
+    early = CHUNK // per
+
+    @pl.when(step == steps - early)
+    def _():
+        wq_copy.wait()
+
+    @pl.when(step >= steps - early)
+    def _():
+        def out(i, head, value):
+            q_ref[i, head] = value
+
+        project_queries(h, wq_ref, cos, sin, out, hd, group, tree)
 
     @pl.when(step == steps - 1)
     def _():
-        for c in flush(step, slot):
-            c.wait()
-
-
-def attend_kernel(ctx_ref, q_hbm, mask_hbm, kc_hbm, vc_hbm, hid_hbm, wo_hbm, out_hbm,
-                  y_ref, kbuf, vbuf, kext, qext, mbuf, scores, msg, rpart, xsend, xrecv, psend, precv, wout, resid, stage,
-                  kv_sem, w_sem, hid_sem, out_sem, snd, rcv):
+        for back in range(slots):
+            for c in flush(steps - 1 - back):
+                c.wait()
+
+
+def attend_kernel(ctx_ref, gain_ref, q_hbm, tab_hbm, mask_hbm, kc_hbm, vc_hbm, hid_hbm, wq_hbm, wo_hbm, out_ref,
+                  y_ref, kbuf, vbuf, kext, qext, mbuf, scores, msg, rpart, xsend, xrecv, psend, precv, wout, resid, wq_ref, xbuf, tbuf, qbuf,
+                  kv_sem, w_sem, hid_sem, q_sem, snd, rcv):
     cp, tp = lax.axis_index('cp'), lax.axis_index('tp')
     chip, core = cp // 2, cp % 2
     partner = {'cp': chip * 2 + 1 - core}
     across_x = {'cp': (1 - chip) * 2 + core}
     across_y = {'tp': 1 - tp}
-    nreq, heads, hd, qcols = q_hbm.shape
+    _, heads, hd, qcols = q_hbm.shape
+    nreq = mask_hbm.shape[0]
     tree = mask_hbm.shape[1]
     group = qcols // tree
     num_blocks, blk = kbuf.shape[1], kbuf.shape[4]
@@ -155,8 +187,7 @@
         r, to = request_of(n), n % 2
         return [pltpu.make_async_copy(kc_hbm.at[r], kbuf.at[to], kv_sem.at[to, 0]),
                 pltpu.make_async_copy(vc_hbm.at[r], vbuf.at[to, :, :, pl.ds(0, hd), :], kv_sem.at[to, 1]),
-                pltpu.make_async_copy(q_hbm.at[r], qext.at[to, :, pl.ds(0, hd), :], kv_sem.at[to, 2]),
-                pltpu.make_async_copy(mask_hbm.at[r], mbuf.at[to], kv_sem.at[to, 3])]
+                pltpu.make_async_copy(mask_hbm.at[r], mbuf.at[to], kv_sem.at[to, 2])]
 
     def weight_copies():
         out = []
@@ -168,21 +199,49 @@
     def resid_copies():
         return [pltpu.make_async_copy(hid_hbm.at[k * CHUNK + cp, :, own_cols], resid.at[k], hid_sem.at[k]) for k in range(chunks)]
 
-    for c in fetch(0):
-        c.start()
-    for c in weight_copies() + resid_copies():
+    first_queries = pltpu.make_async_copy(q_hbm, qbuf.at[0], q_sem.at[0])
+    query_weight = pltpu.make_async_copy(wq_hbm, wq_ref, q_sem.at[1])
+
+    def chunk_copies(k):
+        pairs = tbuf.shape[0]
+        return [pltpu.make_async_copy(hid_hbm.at[pl.ds(k * CHUNK, CHUNK)], xbuf, q_sem.at[2]),
+                pltpu.make_async_copy(tab_hbm.at[pl.ds(k * pairs, pairs)], tbuf, q_sem.at[3])]
+
+    for c in fetch(0) + [first_queries] + chunk_copies(1) + [query_weight] + weight_copies() + resid_copies():
         c.start()
     ones = jnp.ones((vbuf.shape[3] - hd, blk), BF16)
     for s in range(2):
         for j in range(num_blocks):
             for h in range(heads):
                 vbuf[s, j, h, hd:, :] = ones
-    pad = qext.shape[2] - hd - tree
+    pad = qext.shape[1] - hd - tree
     hide = jnp.where(lax.broadcasted_iota(jnp.int32, (pad, qcols), 0) == 0, MASKED, 0.0).astype(BF16)
-    for s in range(2):
-        for h in range(heads):
-            qext[s, h, hd + tree:, :] = hide
+    for h in range(heads):
+        qext[h, hd + tree:, :] = hide
     pl.semaphore_wait(barrier, 3)
+    first_queries.wait()
+
+    def queries(k):
+        for c in chunk_copies(k):
+            c.wait()
+
+        @pl.when(k == 1)
+        def _():
+            query_weight.wait()
+
+        h = normed_rows(xbuf[...].reshape(CHUNK * tree, width), gain_ref[...])
+        cos = jnp.concatenate([tbuf[p, 0] for p in range(tbuf.shape[0])], axis=1)
+        sin = jnp.concatenate([tbuf[p, 1] for p in range(tbuf.shape[0])], axis=1)
+
+        def out(i, head, value):
+            qbuf[k % 2, i, head] = value
+
+        project_queries(h, wq_ref, cos, sin, out, hd, group, tree)
+
+        @pl.when(k + 1 < chunks)
+        def _():
+            for c in chunk_copies(k + 1):
+                c.start()
 
     def attend(n):
         k, r, slot = n // CHUNK, request_of(n), n % 2
@@ -199,7 +258,8 @@
         seen = jnp.concatenate([mbuf[slot].astype(F32)] * group, axis=0).T
         bias = jnp.where(seen > 0.0, 0.0, MASKED).astype(BF16)
         for h in range(heads):
-            qext[slot, h, hd:hd + tree, :] = bias
+            qext[h, :hd, :] = qbuf[k % 2, i, h]
+            qext[h, hd:hd + tree, :] = bias
         late = num_blocks // 2
         for j in range(late, num_blocks):
             off = (j * 4 + cp) * blk - ctx
@@ -215,9 +275,9 @@
 
         def score(h, j):
             if j < late:
-                s = mm_tn(kbuf[slot, j, h], qext[slot, h, :hd, :])
+                s = mm_tn(kbuf[slot, j, h], qext[h, :hd, :])
             else:
-                s = mm_tn(kext[j - late, h], qext[slot, h])
+                s = mm_tn(kext[j - late, h], qext[h])
             scores[h % 2, j * blk:(j + 1) * blk, :] = s
             return jnp.max(s.reshape(blk // 8, 8, qcols), axis=0)
 
@@ -347,38 +407,26 @@
         landed(k, 9)
         gather_copy(k, 12).start()
 
-    def out_copy(k):
-        return pltpu.make_async_copy(stage.at[k % 2], out_hbm.at[pl.ds(k * CHUNK, CHUNK)], out_sem.at[k % 2])
-
     def emit(k):
         for n in (6, 8, 10, 11, 12):
             landed(k, n)
-
-        @pl.when(k >= 2)
-        def _():
-            out_copy(k - 2).wait()
-
         for i in range(CHUNK):
-            stage[k % 2, i] = y_ref[k * CHUNK + i].astype(BF16)
-        out_copy(k).start()
-
-    steps = ((merge_chip, 3), (project, 7), (finish, 11), (forward, 15), (forward_diagonal, 19), (emit, 23))
-
-    @pl.loop(0, nreq + steps[-1][1])
+            out_ref[k * CHUNK + i] = y_ref[k * CHUNK + i].astype(BF16)
+
+    steps = ((merge_chip, 0, 2 + core), (queries, 1, -1), (project, 0, 7), (finish, 0, 11), (forward, 0, 15), (forward_diagonal, 0, 19), (emit, 0, 23))
+
+    @pl.loop(0, nreq + steps[-1][2])
     def _(n):
         @pl.when(n < nreq)
         def _():
             attend(n)
 
-        for work, after in steps:
+        for work, lowest, after in steps:
             since = n + 1 - after
 
-            @pl.when((since >= 0) & (since < nreq) & (since % CHUNK == 0))
+            @pl.when((since >= lowest * CHUNK) & (since < nreq) & (since % CHUNK == 0))
             def _():
                 work(since // CHUNK)
-
-    for k in range(chunks - 2, chunks):
-        out_copy(k).wait()
 
     @pl.loop(0, chunks)
     def _(k):
@@ -400,60 +448,67 @@
         qdim, kvdim = w_query.shape[1], w_key.shape[1]
         group = qdim // kvdim
         chunks = nreq // CHUNK
-        rows = CHUNK * tree
         keys = jnp.swapaxes(cache_k[:, :, 0], -1, -2)
         values = jnp.swapaxes(cache_v[:, :, 0], -1, -2)
         hbm = pl.BlockSpec(memory_space=pl.ANY)
+        vmem = pl.BlockSpec(memory_space=pltpu.VMEM)
         smem = pl.BlockSpec(memory_space=pltpu.SMEM)
         cache_shape = jax.ShapeDtypeStruct(keys.shape, BF16)
-        query, new_keys, new_vals = pl.pallas_call(
-            qkv_kernel,
-            grid=(chunks,),
-            in_specs=[smem, pl.BlockSpec((rows, width), lambda s: (s, 0)), pl.BlockSpec((width,), lambda s: (0,)),
-                      pl.BlockSpec((width, qdim), lambda s: (0, 0)), pl.BlockSpec((width, kvdim), lambda s: (0, 0)), pl.BlockSpec((width, kvdim), lambda s: (0, 0)),
-                      pl.BlockSpec((nreq, tree), lambda s: (0, 0)), pl.BlockSpec((hd // 2, 128), lambda s: (0, 0)), hbm, hbm],
-            out_specs=[pl.BlockSpec((CHUNK, kv_heads, hd, group * tree), lambda s: (s, 0, 0, 0)), hbm, hbm],
-            out_shape=[jax.ShapeDtypeStruct((nreq, kv_heads, hd, group * tree), BF16), cache_shape, cache_shape],
-            scratch_shapes=[pltpu.VMEM((2, 2, CHUNK, num_blocks, kv_heads, hd, blk), BF16), pltpu.VMEM((2, kvdim, rows), BF16),
-                            pltpu.SemaphoreType.DMA((2, 2)), pltpu.SemaphoreType.DMA((2, 2))],
-            compiler_params=pltpu.CompilerParams(vmem_limit_bytes=58 * 2**20),
-            name='qkv_and_cache',
-        )(ctx_len, hidden.reshape(nreq * tree, width), attn_gain, w_query, w_key, w_value, positions, jnp.asarray(rope_frequencies(hd)), keys, values)
+        per, slots = CHUNK // 2, 4
+        steps, early, rows = nreq // per, CHUNK // per, per * tree
         qcols = group * tree
+        query, tables, new_keys, new_vals = pl.pallas_call(
+            cache_kernel,
+            grid=(steps,),
+            in_specs=[smem, pl.BlockSpec((rows, width), lambda s: (steps - 1 - s, 0)), pl.BlockSpec((width,), lambda s: (0,)),
+                      pl.BlockSpec((width, kvdim), lambda s: (0, 0)), pl.BlockSpec((width, kvdim), lambda s: (0, 0)),
+                      pl.BlockSpec((nreq, tree), lambda s: (0, 0)), pl.BlockSpec((hd // 2,), lambda s: (0,)), hbm, hbm, hbm],
+            out_specs=[pl.BlockSpec((per, kv_heads, hd, qcols), lambda s: (jnp.minimum(steps - 1 - s, early - 1), 0, 0, 0)),
+                       pl.BlockSpec((1, 2, hd // 2, rows), lambda s: (steps - 1 - s, 0, 0, 0)), hbm, hbm],
+            out_shape=[jax.ShapeDtypeStruct((CHUNK, kv_heads, hd, qcols), BF16), jax.ShapeDtypeStruct((steps, 2, hd // 2, rows), F32), cache_shape, cache_shape],
+            scratch_shapes=[pltpu.VMEM((slots, 2, per, num_blocks, kv_heads, hd, blk), BF16), pltpu.VMEM((2, kvdim, rows), BF16), pltpu.VMEM((width, qdim), BF16),
+                            pltpu.SemaphoreType.DMA((slots, 2)), pltpu.SemaphoreType.DMA((slots, 2)), pltpu.SemaphoreType.DMA],
+            compiler_params=pltpu.CompilerParams(vmem_limit_bytes=62 * 2**20),
+            name='fill_caches',
+        )(ctx_len, hidden.reshape(nreq * tree, width), attn_gain, w_key, w_value, positions, jnp.asarray(rope_frequencies(hd)), w_query, keys, values)
         rows_msg = kv_heads * hd + 2 * kv_heads
         ext = hd + tree + 16
+        wide_rows = (chunks, tree, width // 2)
         out_hidden = pl.pallas_call(
             attend_kernel,
-            in_specs=[smem, hbm, hbm, hbm, hbm, hbm, hbm],
-            out_specs=hbm,
-            out_shape=jax.ShapeDtypeStruct((nreq, tree, width), BF16),
+            in_specs=[smem, vmem] + [hbm] * 8,
+            out_specs=vmem,
+            out_shape=pltpu.VMEM((nreq, tree, width), BF16),
             scratch_shapes=[
                 pltpu.VMEM((nreq, tree, width), F32),
                 pltpu.VMEM((2, num_blocks, kv_heads, hd, blk), BF16),
                 pltpu.VMEM((2, num_blocks, kv_heads, hd + 16, blk), BF16),
                 pltpu.VMEM((num_blocks - num_blocks // 2, kv_heads, ext, blk), BF16),
-                pltpu.VMEM((2, kv_heads, ext, qcols), BF16),
+                pltpu.VMEM((kv_heads, ext, qcols), BF16),
                 pltpu.VMEM((2, tree, tree), jnp.int32),
                 pltpu.VMEM((2, num_blocks * blk, qcols), F32),
                 pltpu.VMEM((chunks, CHUNK, rows_msg, qcols), F32),
                 pltpu.VMEM((chunks, 2, rows_msg, qcols), F32),
                 pltpu.VMEM((chunks, rows_msg, qcols), F32),
                 pltpu.VMEM((chunks, rows_msg, qcols), F32),
-                pltpu.VMEM((chunks, tree, width // 2), F32),
-                pltpu.VMEM((chunks, tree, width // 2), F32),
+                pltpu.VMEM(wide_rows, F32),
+                pltpu.VMEM(wide_rows, F32),
                 pltpu.VMEM((group, kv_heads * hd, width), BF16),
-                pltpu.VMEM((chunks, tree, width // 2), BF16),
-                pltpu.VMEM((2, CHUNK, tree, width), BF16),
-                pltpu.SemaphoreType.DMA((2, 4)),
+                pltpu.VMEM(wide_rows, BF16),
+                pltpu.VMEM((width, qdim), BF16),
+                pltpu.VMEM((CHUNK, tree, width), BF16),
+                pltpu.VMEM((CHUNK // per, 2, hd // 2, rows), F32),
+                pltpu.VMEM((2, CHUNK, kv_heads, hd, qcols), BF16),
+                pltpu.SemaphoreType.DMA((2, 3)),
                 pltpu.SemaphoreType.DMA((group, kv_heads)),
                 pltpu.SemaphoreType.DMA((chunks,)),
-                pltpu.SemaphoreType.DMA((2,)),
+                pltpu.SemaphoreType.DMA((4,)),
                 pltpu.SemaphoreType.DMA((chunks, 13)),
                 pltpu.SemaphoreType.DMA((chunks, 13)),
             ],
-            compiler_params=pltpu.CompilerParams(collective_id=0, has_side_effects=True, vmem_limit_bytes=62 * 2**20),
+            compiler_params=pltpu.CompilerParams(collective_id=0, has_side_effects=True, vmem_limit_bytes=56 * 2**20),
             name='attend_and_combine',
-        )(ctx_len, query, tree_mask, new_keys, new_vals, hidden, w_out)
+        )(ctx_len, attn_gain, query, tables, tree_mask, new_keys, new_vals, hidden, w_query, w_out)
         return (out_hidden, jnp.swapaxes(new_keys, -1, -2)[:, :, None], jnp.swapaxes(new_vals, -1, -2)[:, :, None])
 
     return jax.shard_map(local_step, mesh=mesh, in_specs=(row_spec, P(), P(None, 'tp'), P(None, 'tp'), P(None, 'tp'), P('tp', None), cache_spec, cache_spec, row_spec, row_spec, row_spec), out_specs=(row_spec, cache_spec, cache_spec), check_vma=False)

time: 153 us -> 148 us (0.967)
  local copies, waits for them, and re-layouts: 7.94 us -> 2.71 us
    unnamed x1, local copies, waits for them, and re-layouts: 6.61 us -> 2.71 us
where the time goes in v2:
time: 148 us
  Pallas kernels  144 us (97%)
  local copies, waits for them, and re-layouts  2.71 us (2%)
    pallas_call x1, Pallas kernels, local_step(): pl.pallas_call(attend_kernel, in_specs=[smem, vmem] + [hbm] * 8, out_spec...  119 us
    pallas_call x1, Pallas kernels, local_step(): pl.pallas_call(cache_kernel, grid=(steps,), in_specs=[smem, pl.BlockSpec(...  25.1 us

profile of v2, /device:TPU:0, one launch (start us, length us, event | category | flops | bytes accessed | tf_op | source)
XLA Modules:
  0.0 147.5 jit_solution(8091971694655535181)
XLA Ops:
  0.6 25.1 %fill_caches.1 = (bf16[4,4,64,256]{3,2,1,0:T(8,128)(2,1)}, f32[12,2,32,128]{3,2,1,0:T(8,128)}, bf16[24,4,4,64,256]{4,3,2,1,0:T(8,128)(2,1)}, bf16[24,4,4,64,256]{4,3,2,1,0:T(8,128)(2,1)}) custom-call(s32[24]{0:T(128)} %ctx_ref.3, bf16[1536,2048]{1,0:T(8,128)(2,1)} %bitcast.17, bf16[2048]{0:T(1024)(128)(2,1)} %gain_ref.3, bf16[2048,256]{1,0:T(8,128)(2,1)} %wk_ref.1, ...), custom_call_target="tpu_custom_call" | custom-call | tf_op jit(solution)/shard_map/fill_caches/pallas_call | solution.py:460
  25.7 119.1 %attend_and_combine.1 = bf16[24,64,2048]{2,1,0:T(8,128)(2,1)S(1)} custom-call(s32[24]{0:T(128)} %ctx_ref.3, bf16[2048]{0:T(1024)(128)(2,1)} %gain_ref.3, bf16[4,4,64,256]{3,2,1,0:T(8,128)(2,1)} %get-tuple-element.7.q_hbm, f32[12,2,32,128]{3,2,1,0:T(8,128)} %get-tuple-element.8.tab_hbm, s32[24,64,64]{2,1,0:T(8,128)} %mask_hbm.1, ...), custom_call_target="tpu_custom_call" | custom-call | tf_op jit(solution)/shard_map/attend_and_combine/pallas_call | solution.py:477
  144.8 2.7 %copy.18 = bf16[24,64,2048]{2,1,0:T(8,128)(2,1)} copy(bf16[24,64,2048]{2,1,0:T(8,128)(2,1)S(1)} %attend_and_combine.1) | data formatting | bytes 12582912

commit v3 on v2

--- a/solution.py
+++ b/solution.py
@@ -16,7 +16,17 @@
 F32 = jnp.float32
 BF16 = jnp.bfloat16
 CHUNK = 4
-
+EARLY_CHUNKS = 3
+
+SCHEDULE = (
+    ('forward', 0, (16, 17, 28, 30, 35, 36)),
+    ('merge', 0, (2, 6, 9, 15, 19, 21)),
+    ('emit', 0, (29, 30, 34, 38, 40, 41)),
+    ('project', 0, (7, 9, 15, 19, 26, 27)),
+    ('query', EARLY_CHUNKS, (9, 14, 18)),
+    ('finish', 0, (9, 13, 21, 25, 31, 33)),
+    ('diagonal', 0, (21, 24, 32, 37, 39, 40)),
+)
 
 def mm(a, b):
     return jnp.dot(a, b, preferred_element_type=F32)
@@ -78,21 +88,22 @@
 
     @pl.when(step == 0)
     def _():
-        for c in fetch(0) + fetch(1):
-            c.start()
-
-    @pl.when(step == 1)
+        for ahead in range(slots // 2):
+            for c in fetch(ahead):
+                c.start()
+
+        wq_copy.start()
+
+    later = step + slots // 2
+
+    @pl.when(later < steps)
     def _():
-        wq_copy.start()
-
-    @pl.when(step + 2 < steps)
-    def _():
-        @pl.when(step + 2 >= slots)
-        def _():
-            for c in flush(step + 2 - slots):
+        @pl.when(later >= slots)
+        def _():
+            for c in flush(later - slots):
                 c.wait()
 
-        for c in fetch(step + 2):
+        for c in fetch(later):
             c.start()
 
     h = normed_rows(x_ref[...], gain_ref[...])
@@ -133,7 +144,7 @@
     for c in flush(step):
         c.start()
 
-    early = CHUNK // per
+    early = EARLY_CHUNKS * CHUNK // per
 
     @pl.when(step == steps - early)
     def _():
@@ -161,7 +172,7 @@
     partner = {'cp': chip * 2 + 1 - core}
     across_x = {'cp': (1 - chip) * 2 + core}
     across_y = {'tp': 1 - tp}
-    _, heads, hd, qcols = q_hbm.shape
+    _, _, heads, hd, qcols = q_hbm.shape
     nreq = mask_hbm.shape[0]
     tree = mask_hbm.shape[1]
     group = qcols // tree
@@ -199,7 +210,7 @@
     def resid_copies():
         return [pltpu.make_async_copy(hid_hbm.at[k * CHUNK + cp, :, own_cols], resid.at[k], hid_sem.at[k]) for k in range(chunks)]
 
-    first_queries = pltpu.make_async_copy(q_hbm, qbuf.at[0], q_sem.at[0])
+    first_queries = pltpu.make_async_copy(q_hbm, qbuf, q_sem.at[0])
     query_weight = pltpu.make_async_copy(wq_hbm, wq_ref, q_sem.at[1])
 
     def chunk_copies(k):
@@ -207,7 +218,7 @@
         return [pltpu.make_async_copy(hid_hbm.at[pl.ds(k * CHUNK, CHUNK)], xbuf, q_sem.at[2]),
                 pltpu.make_async_copy(tab_hbm.at[pl.ds(k * pairs, pairs)], tbuf, q_sem.at[3])]
 
-    for c in fetch(0) + [first_queries] + chunk_copies(1) + [query_weight] + weight_copies() + resid_copies():
+    for c in fetch(0) + [first_queries] + chunk_copies(EARLY_CHUNKS) + [query_weight] + weight_copies() + resid_copies():
         c.start()
     ones = jnp.ones((vbuf.shape[3] - hd, blk), BF16)
     for s in range(2):
@@ -225,7 +236,7 @@
         for c in chunk_copies(k):
             c.wait()
 
-        @pl.when(k == 1)
+        @pl.when(k == EARLY_CHUNKS)
         def _():
             query_weight.wait()
 
@@ -234,7 +245,7 @@
         sin = jnp.concatenate([tbuf[p, 1] for p in range(tbuf.shape[0])], axis=1)
 
         def out(i, head, value):
-            qbuf[k % 2, i, head] = value
+            qbuf[k % EARLY_CHUNKS, i, head] = value
 
         project_queries(h, wq_ref, cos, sin, out, hd, group, tree)
 
@@ -258,7 +269,7 @@
         seen = jnp.concatenate([mbuf[slot].astype(F32)] * group, axis=0).T
         bias = jnp.where(seen > 0.0, 0.0, MASKED).astype(BF16)
         for h in range(heads):
-            qext[h, :hd, :] = qbuf[k % 2, i, h]
+            qext[h, :hd, :] = qbuf[k % EARLY_CHUNKS, i, h]
             qext[h, hd:hd + tree, :] = bias
         late = num_blocks // 2
         for j in range(late, num_blocks):
@@ -351,11 +362,11 @@
 
         psend[k] = part(other_cols)
         remote(psend.at[k], precv.at[k], k, 3, across_y).start()
-        y_ref[k * CHUNK + cp, :, own_cols] = resid[k].astype(F32) + part(own_cols)
+        y_ref[k * CHUNK + cp, tp] = resid[k].astype(F32) + part(own_cols)
 
     def piece(k, owner_cp, owner_tp, lo=0, n=None):
         rows = pl.ds(lo, tree if n is None else n)
-        return y_ref.at[k * CHUNK + owner_cp, rows, pl.ds(pl.multiple_of(owner_tp * wcols, wcols), wcols)]
+        return y_ref.at[k * CHUNK + owner_cp, owner_tp, rows]
 
     hf = (tree * 3 // 8) // 8 * 8
     hb = tree - hf
@@ -388,8 +399,8 @@
 
     def finish(k):
         remote(psend.at[k], precv.at[k], k, 3, across_y).wait_recv()
-        total = y_ref[k * CHUNK + cp, :, own_cols] + precv[k]
-        y_ref[k * CHUNK + cp, :, own_cols] = total.astype(BF16).astype(F32)
+        total = y_ref[k * CHUNK + cp, tp] + precv[k]
+        y_ref[k * CHUNK + cp, tp] = total.astype(BF16).astype(F32)
         for n in (4, 5, 6):
             gather_copy(k, n).start()
 
@@ -411,22 +422,21 @@
         for n in (6, 8, 10, 11, 12):
             landed(k, n)
         for i in range(CHUNK):
-            out_ref[k * CHUNK + i] = y_ref[k * CHUNK + i].astype(BF16)
-
-    steps = ((merge_chip, 0, 2 + core), (queries, 1, -1), (project, 0, 7), (finish, 0, 11), (forward, 0, 15), (forward_diagonal, 0, 19), (emit, 0, 23))
-
-    @pl.loop(0, nreq + steps[-1][2])
+            for side in range(2):
+                out_ref[k * CHUNK + i, :, side * wcols:(side + 1) * wcols] = y_ref[k * CHUNK + i, side].astype(BF16)
+
+    work = {'merge': merge_chip, 'query': queries, 'project': project, 'finish': finish, 'forward': forward, 'diagonal': forward_diagonal, 'emit': emit}
+
+    @pl.loop(0, 1 + max(max(turns) for _, _, turns in SCHEDULE))
     def _(n):
         @pl.when(n < nreq)
         def _():
             attend(n)
 
-        for work, lowest, after in steps:
-            since = n + 1 - after
-
-            @pl.when((since >= lowest * CHUNK) & (since < nreq) & (since % CHUNK == 0))
+        for name, lowest, turns in SCHEDULE:
+            @pl.when(functools.reduce(jnp.logical_or, [n == t for t in turns]))
             def _():
-                work(since // CHUNK)
+                work[name](sum([jnp.where(n > t, 1, 0) for t in turns]) + lowest)
 
     @pl.loop(0, chunks)
     def _(k):
@@ -454,8 +464,8 @@
         vmem = pl.BlockSpec(memory_space=pltpu.VMEM)
         smem = pl.BlockSpec(memory_space=pltpu.SMEM)
         cache_shape = jax.ShapeDtypeStruct(keys.shape, BF16)
-        per, slots = CHUNK // 2, 4
-        steps, early, rows = nreq // per, CHUNK // per, per * tree
+        per, slots = CHUNK // 2, 8
+        steps, early, rows = nreq // per, EARLY_CHUNKS * CHUNK // per, per * tree
         qcols = group * tree
         query, tables, new_keys, new_vals = pl.pallas_call(
             cache_kernel,
@@ -463,9 +473,9 @@
             in_specs=[smem, pl.BlockSpec((rows, width), lambda s: (steps - 1 - s, 0)), pl.BlockSpec((width,), lambda s: (0,)),
                       pl.BlockSpec((width, kvdim), lambda s: (0, 0)), pl.BlockSpec((width, kvdim), lambda s: (0, 0)),
                       pl.BlockSpec((nreq, tree), lambda s: (0, 0)), pl.BlockSpec((hd // 2,), lambda s: (0,)), hbm, hbm, hbm],
-            out_specs=[pl.BlockSpec((per, kv_heads, hd, qcols), lambda s: (jnp.minimum(steps - 1 - s, early - 1), 0, 0, 0)),
+            out_specs=[pl.BlockSpec((pl.squeezed, per, kv_heads, hd, qcols), lambda s: (jnp.minimum(steps - 1 - s, early - 1) // (CHUNK // per), jnp.minimum(steps - 1 - s, early - 1) % (CHUNK // per), 0, 0, 0)),
                        pl.BlockSpec((1, 2, hd // 2, rows), lambda s: (steps - 1 - s, 0, 0, 0)), hbm, hbm],
-            out_shape=[jax.ShapeDtypeStruct((CHUNK, kv_heads, hd, qcols), BF16), jax.ShapeDtypeStruct((steps, 2, hd // 2, rows), F32), cache_shape, cache_shape],
+            out_shape=[jax.ShapeDtypeStruct((EARLY_CHUNKS, CHUNK, kv_heads, hd, qcols), BF16), jax.ShapeDtypeStruct((steps, 2, hd // 2, rows), F32), cache_shape, cache_shape],
             scratch_shapes=[pltpu.VMEM((slots, 2, per, num_blocks, kv_heads, hd, blk), BF16), pltpu.VMEM((2, kvdim, rows), BF16), pltpu.VMEM((width, qdim), BF16),
                             pltpu.SemaphoreType.DMA((slots, 2)), pltpu.SemaphoreType.DMA((slots, 2)), pltpu.SemaphoreType.DMA],
             compiler_params=pltpu.CompilerParams(vmem_limit_bytes=62 * 2**20),
@@ -480,7 +490,7 @@
             out_specs=vmem,
             out_shape=pltpu.VMEM((nreq, tree, width), BF16),
             scratch_shapes=[
-                pltpu.VMEM((nreq, tree, width), F32),
+                pltpu.VMEM((nreq, 2, tree, width // 2), F32),
                 pltpu.VMEM((2, num_blocks, kv_heads, hd, blk), BF16),
                 pltpu.VMEM((2, num_blocks, kv_heads, hd + 16, blk), BF16),
                 pltpu.VMEM((num_blocks - num_blocks // 2, kv_heads, ext, blk), BF16),
@@ -498,7 +508,7 @@
                 pltpu.VMEM((width, qdim), BF16),
                 pltpu.VMEM((CHUNK, tree, width), BF16),
                 pltpu.VMEM((CHUNK // per, 2, hd // 2, rows), F32),
-                pltpu.VMEM((2, CHUNK, kv_heads, hd, qcols), BF16),
+                pltpu.VMEM((EARLY_CHUNKS, CHUNK, kv_heads, hd, qcols), BF16),
                 pltpu.SemaphoreType.DMA((2, 3)),
                 pltpu.SemaphoreType.DMA((group, kv_heads)),
                 pltpu.SemaphoreType.DMA((chunks,)),

time: 148 us -> 147 us (level)
    pallas_call x1, Pallas kernels: 119 us -> 116 us  [local_step(): pl.pallas_call(attend_kernel, in_specs=[smem, vmem] + [hbm] * 8, out_spec...]
    pallas_call x1, Pallas kernels: 25.1 us -> 27.4 us  [local_step(): pl.pallas_call(cache_kernel, grid=(steps,), in_specs=[smem, pl.BlockSpec(...]
where the time goes in v3:
time: 147 us; the launch traced here: 146 us
  Pallas kernels  143 us (97%)
  local copies, waits for them, and re-layouts  2.71 us (2%)
    pallas_call x1, Pallas kernels, local_step(): pl.pallas_call(attend_kernel, in_specs=[smem, vmem] + [hbm] * 8, out_spec...  116 us
    pallas_call x1, Pallas kernels, local_step(): pl.pallas_call(cache_kernel, grid=(steps,), in_specs=[smem, pl.BlockSpec(...  27.4 us

profile of v3, /device:TPU:0, one launch (start us, length us, event | category | flops | bytes accessed | tf_op | source)
XLA Modules:
  0.0 146.4 jit_solution(12216680696820244560)
XLA Ops:
  0.6 27.4 %fill_caches.1 = (bf16[3,4,4,64,256]{4,3,2,1,0:T(8,128)(2,1)}, f32[12,2,32,128]{3,2,1,0:T(8,128)}, bf16[24,4,4,64,256]{4,3,2,1,0:T(8,128)(2,1)}, bf16[24,4,4,64,256]{4,3,2,1,0:T(8,128)(2,1)}) custom-call(s32[24]{0:T(128)} %ctx_ref.3, bf16[1536,2048]{1,0:T(8,128)(2,1)} %bitcast.17, bf16[2048]{0:T(1024)(128)(2,1)} %gain_ref.3, bf16[2048,256]{1,0:T(8,128)(2,1)} %wk_ref.1, ...), custom_call_target="tpu_custom_call" | custom-call | tf_op jit(solution)/shard_map/fill_caches/pallas_call | solution.py:470
  28.1 115.6 %attend_and_combine.1 = bf16[24,64,2048]{2,1,0:T(8,128)(2,1)S(1)} custom-call(s32[24]{0:T(128)} %ctx_ref.3, bf16[2048]{0:T(1024)(128)(2,1)} %gain_ref.3, bf16[3,4,4,64,256]{4,3,2,1,0:T(8,128)(2,1)} %get-tuple-element.7.q_hbm, f32[12,2,32,128]{3,2,1,0:T(8,128)} %get-tuple-element.8.tab_hbm, s32[24,64,64]{2,1,0:T(8,128)} %mask_hbm.1, ...), custom_call_target="tpu_custom_call" | custom-call | tf_op jit(solution)/shard_map/attend_and_combine/pallas_call | solution.py:487
  143.6 2.7 %copy.18 = bf16[24,64,2048]{2,1,0:T(8,128)(2,1)} copy(bf16[24,64,2048]{2,1,0:T(8,128)(2,1)S(1)} %attend_and_combine.1) | data formatting | bytes 12582912

commit v4 on v3

--- a/solution.py
+++ b/solution.py
@@ -17,15 +17,16 @@
 BF16 = jnp.bfloat16
 CHUNK = 4
 EARLY_CHUNKS = 3
+HEAD_STEPS = 3
 
 SCHEDULE = (
-    ('forward', 0, (16, 17, 28, 30, 35, 36)),
-    ('merge', 0, (2, 6, 9, 15, 19, 21)),
-    ('emit', 0, (29, 30, 34, 38, 40, 41)),
-    ('project', 0, (7, 9, 15, 19, 26, 27)),
-    ('query', EARLY_CHUNKS, (9, 14, 18)),
-    ('finish', 0, (9, 13, 21, 25, 31, 33)),
-    ('diagonal', 0, (21, 24, 32, 37, 39, 40)),
+    ('emit', 0, (29, 31, 35, 36, 37, 38)),
+    ('diagonal', 0, (22, 29, 30, 33, 34, 35)),
+    ('forward', 0, (15, 17, 26, 30, 31, 32)),
+    ('project', 0, (9, 10, 17, 19, 24, 25)),
+    ('query', EARLY_CHUNKS, (9, 14, 16)),
+    ('merge', 0, (4, 7, 9, 15, 19, 21)),
+    ('finish', 0, (10, 13, 21, 24, 27, 28)),
 )
 
 def mm(a, b):
@@ -45,6 +46,18 @@
     return np.where(wavelen < 2048.0, inv_freq, np.where(wavelen > 8192.0, inv_freq / np.float32(8.0), blended)).astype(np.float32)
 
 
+def cos_sin(angle):
+    turns = jnp.floor(angle * (2.0 / math.pi) + 0.5)
+    r = ((angle - turns * 1.5703125) - turns * 4.837512969970703125e-4) - turns * 7.549789954891882e-8
+    z = r * r
+    sin_r = r + r * z * (-1.6666654611e-1 + z * (8.3321608736e-3 + z * -1.9515295891e-4))
+    cos_r = 1.0 - 0.5 * z + z * z * (4.166664568298827e-2 + z * (-1.388731625493765e-3 + z * 2.443315711809948e-5))
+    quarter = turns.astype(jnp.int32) & 3
+    odd = (quarter & 1) == 1
+    cos, sin = jnp.where(odd, sin_r, cos_r), jnp.where(odd, cos_r, sin_r)
+    return jnp.where((quarter == 1) | (quarter == 2), -cos, cos), jnp.where(quarter >= 2, -sin, sin)
+
+
 def normed_rows(x, gain):
     wide = x.astype(F32)
     inv_rms = lax.rsqrt(jnp.mean(wide * wide, axis=-1, keepdims=True) + NORM_EPS)
@@ -66,105 +79,185 @@
             out(i, head, jnp.concatenate([p[:, i * tree:(i + 1) * tree] for p in parts], axis=1).astype(BF16))
 
 
-def cache_kernel(ctx_ref, x_ref, gain_ref, wk_ref, wv_ref, pos_ref, freq_ref, wq_hbm, kc_hbm, vc_hbm,
-                 q_ref, tab_ref, ko_hbm, vo_hbm, buf, new_ref, wq_ref, in_sem, out_sem, w_sem):
-    step, steps = pl.program_id(0), pl.num_programs(0)
+def prepare(vref, qext, hd, tree):
+    num_blocks, heads, vrows, blk = vref.shape
+    ones = jnp.ones((vrows - hd, blk), BF16)
+    pad = qext.shape[1] - hd - tree
+    hide = jnp.where(lax.broadcasted_iota(jnp.int32, (pad, qext.shape[2]), 0) == 0, MASKED, 0.0).astype(BF16)
+    for h in range(heads):
+        for j in range(num_blocks):
+            vref[j, h, hd:, :] = ones
+        qext[h, hd + tree:, :] = hide
+
+
+def attention(ctx, tree_mask, qref, kref, vref, kext, qext, scores, out, cp):
+    num_blocks, heads, hd, blk = kref.shape
+    qcols, tree = qext.shape[2], tree_mask.shape[0]
+    pad = qext.shape[1] - hd - tree
+    late = num_blocks // 2
+    coef = hd ** -0.5 * LOG2E
+    seen = jnp.concatenate([tree_mask.astype(F32)] * (qcols // tree), axis=0).T
+    bias = jnp.where(seen > 0.0, 0.0, MASKED).astype(BF16)
+    for h in range(heads):
+        qext[h, :hd, :] = qref[h]
+        qext[h, hd:hd + tree, :] = bias
+    for j in range(late, num_blocks):
+        off = (j * 4 + cp) * blk - ctx
+        tok = off + lax.broadcasted_iota(jnp.int32, (tree, blk), 1)
+        pick = jnp.where(tok == lax.broadcasted_iota(jnp.int32, (tree, blk), 0), 1.0, 0.0).astype(BF16)
+        tok_p = off + lax.broadcasted_iota(jnp.int32, (pad, blk), 1)
+        tail = jnp.where((tok_p >= tree) & (lax.broadcasted_iota(jnp.int32, (pad, blk), 0) == 0), 1.0, 0.0).astype(BF16)
+        tok_h = off + lax.broadcasted_iota(jnp.int32, (hd, blk), 1)
+        for h in range(heads):
+            kext[j - late, h, :hd, :] = jnp.where(tok_h < tree, kref[j, h].astype(F32), 0.0).astype(BF16)
+            kext[j - late, h, hd:hd + tree, :] = pick
+            kext[j - late, h, hd + tree:, :] = tail
+
+    def score(h, j):
+        if j < late:
+            s = mm_tn(kref[j, h], qext[h, :hd, :])
+        else:
+            s = mm_tn(kext[j - late, h], qext[h])
+        scores[h % 2, j * blk:(j + 1) * blk, :] = s
+        return jnp.max(s.reshape(blk // 8, 8, qcols), axis=0)
+
+    tops = [None] * heads
+    tops[0] = functools.reduce(jnp.maximum, [score(0, j) for j in range(num_blocks)])
+    for h in range(heads):
+        top = jnp.max(tops[h], axis=0, keepdims=True)
+        shift = top * coef
+        total, nxt = None, []
+        for j in range(num_blocks):
+            if h + 1 < heads:
+                nxt.append(score(h + 1, j))
+            p = jnp.exp2(scores[h % 2, j * blk:(j + 1) * blk, :] * coef - shift).astype(BF16)
+            o = mm(vref[j, h], p)
+            total = o if total is None else total + o
+        if h + 1 < heads:
+            tops[h + 1] = functools.reduce(jnp.maximum, nxt)
+        out[h * hd:(h + 1) * hd, :] = total[:hd]
+        out[heads * hd + h:heads * hd + h + 1, :] = top
+        out[heads * hd + heads + h:heads * hd + heads + h + 1, :] = total[hd:hd + 1]
+
+
+def cache_kernel(ctx_ref, gain_ref, pos_ref, freq_ref, mask_ref, wk_hbm, wv_hbm, wq_hbm, x_hbm, kc_hbm, vc_hbm,
+                 q_ref, tab_ref, msg_hbm, ko_hbm, vo_hbm,
+                 buf, xbuf, new_ref, wk_ref, wv_ref, wq_ref, vbuf, kext, qext, scores, msg, in_sem, out_sem, w_sem, msg_sem):
     cp_rank, cp_size = lax.axis_index('cp'), lax.axis_size('cp')
     slots, _, per, num_blocks, kv_heads, hd, blk = buf.shape
-    slot = lax.rem(step, slots)
-    tree = pos_ref.shape[1]
-    group = q_ref.shape[3] // tree
-    first_req = (steps - 1 - step) * per
+    nreq, tree = pos_ref.shape
+    steps = nreq // per
+    group = q_ref.shape[4] // tree
+    width = x_hbm.shape[2]
+    half = hd // 2
+    cols = per * tree
+
+    def pair_of(idx):
+        return (idx + steps - HEAD_STEPS) % steps
 
     def fetch(idx):
-        rows, to = pl.ds((steps - 1 - idx) * per, per), lax.rem(idx, slots)
-        return [pltpu.make_async_copy(src.at[rows], buf.at[to, n], in_sem.at[to, n]) for n, src in enumerate((kc_hbm, vc_hbm))]
+        rows, to = pl.ds(pair_of(idx) * per, per), idx % slots
+        return [pltpu.make_async_copy(x_hbm.at[rows], xbuf.at[to], in_sem.at[to, 2])] + [
+            pltpu.make_async_copy(src.at[rows], buf.at[to, n], in_sem.at[to, n]) for n, src in enumerate((kc_hbm, vc_hbm))]
 
     def flush(idx):
-        rows, frm = pl.ds((steps - 1 - idx) * per, per), lax.rem(idx, slots)
+        rows, frm = pl.ds(pair_of(idx) * per, per), idx % slots
         return [pltpu.make_async_copy(buf.at[frm, n], dst.at[rows], out_sem.at[frm, n]) for n, dst in enumerate((ko_hbm, vo_hbm))]
 
-    wq_copy = pltpu.make_async_copy(wq_hbm, wq_ref, w_sem)
-
-    @pl.when(step == 0)
-    def _():
-        for ahead in range(slots // 2):
-            for c in fetch(ahead):
-                c.start()
-
-        wq_copy.start()
-
-    later = step + slots // 2
-
-    @pl.when(later < steps)
-    def _():
-        @pl.when(later >= slots)
-        def _():
-            for c in flush(later - slots):
-                c.wait()
-
-        for c in fetch(later):
+    kv_weights = [pltpu.make_async_copy(src, dst, w_sem.at[n]) for n, (src, dst) in enumerate(((wk_hbm, wk_ref), (wv_hbm, wv_ref)))]
+    q_weight = pltpu.make_async_copy(wq_hbm, wq_ref, w_sem.at[2])
+    ahead = slots // 2
+    for c in fetch(0) + kv_weights:
+        c.start()
+    for idx in range(1, ahead):
+        for c in fetch(idx):
             c.start()
-
-    h = normed_rows(x_ref[...], gain_ref[...])
-    half = hd // 2
+    q_weight.start()
+    prepare(vbuf, qext, hd, tree)
     diag = lax.broadcasted_iota(jnp.int32, (half, half), 0) == lax.broadcasted_iota(jnp.int32, (half, half), 1)
     freq = jnp.sum(jnp.where(diag, freq_ref[...][None, :], 0.0), axis=1, keepdims=True)
-    pos = jnp.concatenate([pos_ref[pl.ds(first_req + i, 1), :] for i in range(per)], axis=1).astype(F32)
-    angle = pos * freq
-    cos, sin = jnp.cos(angle), jnp.sin(angle)
-    tab_ref[0, 0] = cos
-    tab_ref[0, 1] = sin
-    key_t = mm(h, wk_ref[...]).T
-    for n in range(kv_heads):
-        new_ref[0, n * hd:(n + 1) * hd, :] = rotate(key_t[n * hd:(n + 1) * hd], cos, sin).astype(BF16)
-    new_ref[1] = mm(h, wv_ref[...]).T.astype(BF16)
-
-    for c in fetch(step):
+    for c in kv_weights:
         c.wait()
-    cols = per * tree
-    for i in range(per):
-        ctx = ctx_ref[first_req + i]
-        for j in range(num_blocks // 2, num_blocks):
-            first_pos = (j * cp_size + cp_rank) * blk
-
-            @pl.when((first_pos < ctx + tree) & (first_pos + blk > ctx))
+
+    @pl.loop(0, steps)
+    def _(step):
+        slot, pair = step % slots, pair_of(step)
+        later = step + ahead
+
+        @pl.when(later < steps)
+        def _():
+            @pl.when(later >= slots)
             def _():
-                tok = first_pos - ctx + lax.broadcasted_iota(jnp.int32, (cols, blk), 1)
-                row = lax.broadcasted_iota(jnp.int32, (cols, blk), 0) - i * tree
-                pick = jnp.where((row == tok) & (row >= 0) & (row < tree), 1.0, 0.0).astype(BF16)
-                tok_h = first_pos - ctx + lax.broadcasted_iota(jnp.int32, (hd, blk), 1)
-                fresh = (tok_h >= 0) & (tok_h < tree)
-                for n in range(2):
-                    put = mm(new_ref[n], pick)
+                for c in flush(later - slots):
+                    c.wait()
+
+            for c in fetch(later):
+                c.start()
+
+        for c in fetch(step):
+            c.wait()
+        h = normed_rows(xbuf[slot].reshape(cols, width), gain_ref[...])
+        pos = jnp.concatenate([pos_ref[pl.ds(pair * per + i, 1), :] for i in range(per)], axis=1).astype(F32)
+        cos, sin = cos_sin(pos * freq)
+        tab_ref[pair, 0] = cos
+        tab_ref[pair, 1] = sin
+        key_t = mm(h, wk_ref[...]).T
+        for n in range(kv_heads):
+            new_ref[0, n * hd:(n + 1) * hd, :] = rotate(key_t[n * hd:(n + 1) * hd], cos, sin).astype(BF16)
+        new_ref[1] = mm(h, wv_ref[...]).T.astype(BF16)
+        for i in range(per):
+            ctx = ctx_ref[pair * per + i]
+            for j in range(num_blocks // 2, num_blocks):
+                first_pos = (j * cp_size + cp_rank) * blk
+
+                @pl.when((first_pos < ctx + tree) & (first_pos + blk > ctx))
+                def _():
+                    tok = first_pos - ctx + lax.broadcasted_iota(jnp.int32, (cols, blk), 1)
+                    row = lax.broadcasted_iota(jnp.int32, (cols, blk), 0) - i * tree
+                    pick = jnp.where((row == tok) & (row >= 0) & (row < tree), 1.0, 0.0).astype(BF16)
+                    tok_h = first_pos - ctx + lax.broadcasted_iota(jnp.int32, (hd, blk), 1)
+                    fresh = (tok_h >= 0) & (tok_h < tree)
+                    for n in range(2):
+                        put = mm(new_ref[n], pick)
+                        for head in range(kv_heads):
+                            old = buf[slot, n, i, j, head].astype(F32)
+                            buf[slot, n, i, j, head] = jnp.where(fresh, put[head * hd:(head + 1) * hd], old).astype(BF16)
+
+        for c in flush(step):
+            c.start()
+
+        @pl.when(step == HEAD_STEPS)
+        def _():
+            q_weight.wait()
+
+        @pl.when(pair < EARLY_CHUNKS * CHUNK // per)
+        def _():
+            req = pair * per
+
+            def out(i, head, value):
+                q_ref[req // CHUNK, req % CHUNK + i, head] = value
+
+            project_queries(h, wq_ref, cos, sin, out, hd, group, tree)
+
+        @pl.when(pair < CHUNK // per)
+        def _():
+            @pl.loop(0, per)
+            def _(i):
+                req = pair * per + i
+                for j in range(num_blocks):
                     for head in range(kv_heads):
-                        old = buf[slot, n, i, j, head].astype(F32)
-                        buf[slot, n, i, j, head] = jnp.where(fresh, put[head * hd:(head + 1) * hd], old).astype(BF16)
-
-    for c in flush(step):
-        c.start()
-
-    early = EARLY_CHUNKS * CHUNK // per
-
-    @pl.when(step == steps - early)
-    def _():
-        wq_copy.wait()
-
-    @pl.when(step >= steps - early)
-    def _():
-        def out(i, head, value):
-            q_ref[i, head] = value
-
-        project_queries(h, wq_ref, cos, sin, out, hd, group, tree)
-
-    @pl.when(step == steps - 1)
-    def _():
-        for back in range(slots):
-            for c in flush(steps - 1 - back):
-                c.wait()
-
-
-def attend_kernel(ctx_ref, gain_ref, q_hbm, tab_hbm, mask_hbm, kc_hbm, vc_hbm, hid_hbm, wq_hbm, wo_hbm, out_ref,
+                        vbuf[j, head, :hd, :] = buf[slot, 1, i, j, head]
+                attention(ctx_ref[req], mask_ref[req], q_ref.at[0, req], buf.at[slot, 0, i], vbuf, kext, qext, scores, msg.at[req], cp_rank)
+                pltpu.make_async_copy(msg.at[req], msg_hbm.at[req], msg_sem.at[req]).start()
+
+    for idx in range(steps - slots, steps):
+        for c in flush(idx):
+            c.wait()
+    for req in range(CHUNK):
+        pltpu.make_async_copy(msg.at[req], msg_hbm.at[req], msg_sem.at[req]).wait()
+
+
+def attend_kernel(ctx_ref, gain_ref, q_hbm, tab_hbm, msg_hbm, mask_hbm, kc_hbm, vc_hbm, hid_hbm, wq_hbm, wo_hbm, out_ref,
                   y_ref, kbuf, vbuf, kext, qext, mbuf, scores, msg, rpart, xsend, xrecv, psend, precv, wout, resid, wq_ref, xbuf, tbuf, qbuf,
                   kv_sem, w_sem, hid_sem, q_sem, snd, rcv):
     cp, tp = lax.axis_index('cp'), lax.axis_index('tp')
@@ -218,18 +311,23 @@
         return [pltpu.make_async_copy(hid_hbm.at[pl.ds(k * CHUNK, CHUNK)], xbuf, q_sem.at[2]),
                 pltpu.make_async_copy(tab_hbm.at[pl.ds(k * pairs, pairs)], tbuf, q_sem.at[3])]
 
-    for c in fetch(0) + [first_queries] + chunk_copies(EARLY_CHUNKS) + [query_weight] + weight_copies() + resid_copies():
+    first_msgs = pltpu.make_async_copy(msg_hbm, msg.at[0], q_sem.at[4])
+    for c in [first_msgs] + fetch(CHUNK) + [first_queries]:
         c.start()
-    ones = jnp.ones((vbuf.shape[3] - hd, blk), BF16)
-    for s in range(2):
-        for j in range(num_blocks):
-            for h in range(heads):
-                vbuf[s, j, h, hd:, :] = ones
-    pad = qext.shape[1] - hd - tree
-    hide = jnp.where(lax.broadcasted_iota(jnp.int32, (pad, qcols), 0) == 0, MASKED, 0.0).astype(BF16)
-    for h in range(heads):
-        qext[h, hd + tree:, :] = hide
+    for to in range(2):
+        prepare(vbuf.at[to], qext, hd, tree)
     pl.semaphore_wait(barrier, 3)
+    first_msgs.wait()
+
+    def share(k, i, which):
+        @pl.when(i % 2 != core)
+        def _():
+            remote(msg.at[k, i], rpart.at[k, which], k, which, partner).start()
+
+    for n in range(CHUNK):
+        share(0, (2 * (1 - chip) + n) % CHUNK, n // 2)
+    for c in weight_copies() + resid_copies() + chunk_copies(EARLY_CHUNKS) + [query_weight]:
+        c.start()
     first_queries.wait()
 
     def queries(k):
@@ -266,55 +364,9 @@
         ctx = ctx_ref[r]
         for c in fetch(n):
             c.wait()
-        seen = jnp.concatenate([mbuf[slot].astype(F32)] * group, axis=0).T
-        bias = jnp.where(seen > 0.0, 0.0, MASKED).astype(BF16)
-        for h in range(heads):
-            qext[h, :hd, :] = qbuf[k % EARLY_CHUNKS, i, h]
-            qext[h, hd:hd + tree, :] = bias
-        late = num_blocks // 2
-        for j in range(late, num_blocks):
-            off = (j * 4 + cp) * blk - ctx
-            tok = off + lax.broadcasted_iota(jnp.int32, (tree, blk), 1)
-            pick = jnp.where(tok == lax.broadcasted_iota(jnp.int32, (tree, blk), 0), 1.0, 0.0).astype(BF16)
-            tok_p = off + lax.broadcasted_iota(jnp.int32, (pad, blk), 1)
-            tail = jnp.where((tok_p >= tree) & (lax.broadcasted_iota(jnp.int32, (pad, blk), 0) == 0), 1.0, 0.0).astype(BF16)
-            tok_h = off + lax.broadcasted_iota(jnp.int32, (hd, blk), 1)
-            for h in range(heads):
-                kext[j - late, h, :hd, :] = jnp.where(tok_h < tree, kbuf[slot, j, h].astype(F32), 0.0).astype(BF16)
-                kext[j - late, h, hd:hd + tree, :] = pick
-                kext[j - late, h, hd + tree:, :] = tail
-
-        def score(h, j):
-            if j < late:
-                s = mm_tn(kbuf[slot, j, h], qext[h, :hd, :])
-            else:
-                s = mm_tn(kext[j - late, h], qext[h])
-            scores[h % 2, j * blk:(j + 1) * blk, :] = s
-            return jnp.max(s.reshape(blk // 8, 8, qcols), axis=0)
-
-        tops = [None] * heads
-        tops[0] = functools.reduce(jnp.maximum, [score(0, j) for j in range(num_blocks)])
-        for h in range(heads):
-            top = jnp.max(tops[h], axis=0, keepdims=True)
-            shift = top * coef
-            total, nxt = None, []
-            for j in range(num_blocks):
-                if h + 1 < heads:
-                    nxt.append(score(h + 1, j))
-                p = jnp.exp2(scores[h % 2, j * blk:(j + 1) * blk, :] * coef - shift).astype(BF16)
-                o = mm(vbuf[slot, j, h], p)
-                total = o if total is None else total + o
-            if h + 1 < heads:
-                tops[h + 1] = functools.reduce(jnp.maximum, nxt)
-            msg[k, i, h * hd:(h + 1) * hd, :] = total[:hd]
-            msg[k, i, heads * hd + h:heads * hd + h + 1, :] = top
-            msg[k, i, heads * hd + heads + h:heads * hd + heads + h + 1, :] = total[hd:hd + 1]
-
-        which = (n % CHUNK) // 2
-
-        @pl.when(i % 2 != core)
-        def _():
-            remote(msg.at[k, i], rpart.at[k, which], k, which, partner).start()
+        attention(ctx, mbuf[slot], qbuf.at[k % EARLY_CHUNKS, i], kbuf.at[slot], vbuf.at[slot], kext, qext, scores, msg.at[k, i], cp)
+
+        share(k, i, (n % CHUNK) // 2)
 
     stat = heads * hd
 
@@ -427,7 +479,7 @@
 
     work = {'merge': merge_chip, 'query': queries, 'project': project, 'finish': finish, 'forward': forward, 'diagonal': forward_diagonal, 'emit': emit}
 
-    @pl.loop(0, 1 + max(max(turns) for _, _, turns in SCHEDULE))
+    @pl.loop(CHUNK, 1 + max(max(turns) for _, _, turns in SCHEDULE))
     def _(n):
         @pl.when(n < nreq)
         def _():
@@ -465,35 +517,48 @@
         smem = pl.BlockSpec(memory_space=pltpu.SMEM)
         cache_shape = jax.ShapeDtypeStruct(keys.shape, BF16)
         per, slots = CHUNK // 2, 8
-        steps, early, rows = nreq // per, EARLY_CHUNKS * CHUNK // per, per * tree
+        steps, rows = nreq // per, per * tree
         qcols = group * tree
-        query, tables, new_keys, new_vals = pl.pallas_call(
+        rows_msg = kv_heads * hd + 2 * kv_heads
+        ext = hd + tree + 16
+        late_blocks = num_blocks - num_blocks // 2
+        query, tables, first_msgs, new_keys, new_vals = pl.pallas_call(
             cache_kernel,
-            grid=(steps,),
-            in_specs=[smem, pl.BlockSpec((rows, width), lambda s: (steps - 1 - s, 0)), pl.BlockSpec((width,), lambda s: (0,)),
-                      pl.BlockSpec((width, kvdim), lambda s: (0, 0)), pl.BlockSpec((width, kvdim), lambda s: (0, 0)),
-                      pl.BlockSpec((nreq, tree), lambda s: (0, 0)), pl.BlockSpec((hd // 2,), lambda s: (0,)), hbm, hbm, hbm],
-            out_specs=[pl.BlockSpec((pl.squeezed, per, kv_heads, hd, qcols), lambda s: (jnp.minimum(steps - 1 - s, early - 1) // (CHUNK // per), jnp.minimum(steps - 1 - s, early - 1) % (CHUNK // per), 0, 0, 0)),
-                       pl.BlockSpec((1, 2, hd // 2, rows), lambda s: (steps - 1 - s, 0, 0, 0)), hbm, hbm],
-            out_shape=[jax.ShapeDtypeStruct((EARLY_CHUNKS, CHUNK, kv_heads, hd, qcols), BF16), jax.ShapeDtypeStruct((steps, 2, hd // 2, rows), F32), cache_shape, cache_shape],
-            scratch_shapes=[pltpu.VMEM((slots, 2, per, num_blocks, kv_heads, hd, blk), BF16), pltpu.VMEM((2, kvdim, rows), BF16), pltpu.VMEM((width, qdim), BF16),
-                            pltpu.SemaphoreType.DMA((slots, 2)), pltpu.SemaphoreType.DMA((slots, 2)), pltpu.SemaphoreType.DMA],
+            in_specs=[smem] + [vmem] * 4 + [hbm] * 6,
+            out_specs=[vmem, vmem, hbm, hbm, hbm],
+            out_shape=[jax.ShapeDtypeStruct((EARLY_CHUNKS, CHUNK, kv_heads, hd, qcols), BF16), jax.ShapeDtypeStruct((steps, 2, hd // 2, rows), F32),
+                       jax.ShapeDtypeStruct((CHUNK, rows_msg, qcols), F32), cache_shape, cache_shape],
+            scratch_shapes=[
+                pltpu.VMEM((slots, 2, per, num_blocks, kv_heads, hd, blk), BF16),
+                pltpu.VMEM((slots, per, tree, width), BF16),
+                pltpu.VMEM((2, kvdim, rows), BF16),
+                pltpu.VMEM((width, kvdim), BF16),
+                pltpu.VMEM((width, kvdim), BF16),
+                pltpu.VMEM((width, qdim), BF16),
+                pltpu.VMEM((num_blocks, kv_heads, hd + 16, blk), BF16),
+                pltpu.VMEM((late_blocks, kv_heads, ext, blk), BF16),
+                pltpu.VMEM((kv_heads, ext, qcols), BF16),
+                pltpu.VMEM((2, num_blocks * blk, qcols), F32),
+                pltpu.VMEM((CHUNK, rows_msg, qcols), F32),
+                pltpu.SemaphoreType.DMA((slots, 3)),
+                pltpu.SemaphoreType.DMA((slots, 2)),
+                pltpu.SemaphoreType.DMA((3,)),
+                pltpu.SemaphoreType.DMA((CHUNK,)),
+            ],
             compiler_params=pltpu.CompilerParams(vmem_limit_bytes=62 * 2**20),
             name='fill_caches',
-        )(ctx_len, hidden.reshape(nreq * tree, width), attn_gain, w_key, w_value, positions, jnp.asarray(rope_frequencies(hd)), w_query, keys, values)
-        rows_msg = kv_heads * hd + 2 * kv_heads
-        ext = hd + tree + 16
+        )(ctx_len, attn_gain, positions, jnp.asarray(rope_frequencies(hd)), tree_mask, w_key, w_value, w_query, hidden, keys, values)
         wide_rows = (chunks, tree, width // 2)
         out_hidden = pl.pallas_call(
             attend_kernel,
-            in_specs=[smem, vmem] + [hbm] * 8,
+            in_specs=[smem, vmem] + [hbm] * 9,
             out_specs=vmem,
             out_shape=pltpu.VMEM((nreq, tree, width), BF16),
             scratch_shapes=[
                 pltpu.VMEM((nreq, 2, tree, width // 2), F32),
                 pltpu.VMEM((2, num_blocks, kv_heads, hd, blk), BF16),
                 pltpu.VMEM((2, num_blocks, kv_heads, hd + 16, blk), BF16),
-                pltpu.VMEM((num_blocks - num_blocks // 2, kv_heads, ext, blk), BF16),
+                pltpu.VMEM((late_blocks, kv_heads, ext, blk), BF16),
                 pltpu.VMEM((kv_heads, ext, qcols), BF16),
                 pltpu.VMEM((2, tree, tree), jnp.int32),
                 pltpu.VMEM((2, num_blocks * blk, qcols), F32),
@@ -512,13 +577,13 @@
                 pltpu.SemaphoreType.DMA((2, 3)),
                 pltpu.SemaphoreType.DMA((group, kv_heads)),
                 pltpu.SemaphoreType.DMA((chunks,)),
-                pltpu.SemaphoreType.DMA((4,)),
+                pltpu.SemaphoreType.DMA((5,)),
                 pltpu.SemaphoreType.DMA((chunks, 13)),
                 pltpu.SemaphoreType.DMA((chunks, 13)),
             ],
             compiler_params=pltpu.CompilerParams(collective_id=0, has_side_effects=True, vmem_limit_bytes=56 * 2**20),
             name='attend_and_combine',
-        )(ctx_len, attn_gain, query, tables, tree_mask, new_keys, new_vals, hidden, w_query, w_out)
+        )(ctx_len, attn_gain, query, tables, first_msgs, tree_mask, new_keys, new_vals, hidden, w_query, w_out)
         return (out_hidden, jnp.swapaxes(new_keys, -1, -2)[:, :, None], jnp.swapaxes(new_vals, -1, -2)[:, :, None])
 
     return jax.shard_map(local_step, mesh=mesh, in_specs=(row_spec, P(), P(None, 'tp'), P(None, 'tp'), P(None, 'tp'), P('tp', None), cache_spec, cache_spec, row_spec, row_spec, row_spec), out_specs=(row_spec, cache_spec, cache_spec), check_vma=False)

time: 147 us -> 143 us (0.973)
  Pallas kernels: 143 us -> 140 us
    pallas_call x2, Pallas kernels: 143 us -> 140 us  [the longest x1 107 us: local_step(): pl.pallas_call(attend_kernel, in_specs=[smem, vmem] + [hbm] * 9, out_spec...]
where the time goes in v4:
time: 143 us
  Pallas kernels  140 us (98%)
  local copies, waits for them, and re-layouts  2.71 us (2%)
    pallas_call x1, Pallas kernels, local_step(): pl.pallas_call(attend_kernel, in_specs=[smem, vmem] + [hbm] * 9, out_spec...  107 us
    pallas_call x1, Pallas kernels, local_step(): pl.pallas_call(cache_kernel, in_specs=[smem] + [vmem] * 4 + [hbm] * 6, ou...  32.6 us

profile of v4, /device:TPU:0, one launch (start us, length us, event | category | flops | bytes accessed | tf_op | source)
XLA Modules:
  0.0 143.1 jit_solution(18091371355208582239)
XLA Ops:
  0.6 32.6 %fill_caches.1 = (bf16[3,4,4,64,256]{4,3,2,1,0:T(8,128)(2,1)}, f32[12,2,32,128]{3,2,1,0:T(8,128)}, f32[4,264,256]{2,1,0:T(8,128)}, bf16[24,4,4,64,256]{4,3,2,1,0:T(8,128)(2,1)}, bf16[24,4,4,64,256]{4,3,2,1,0:T(8,128)(2,1)}) custom-call(s32[24]{0:T(128)} %ctx_ref.3, bf16[2048]{0:T(1024)(128)(2,1)} %gain_ref.3, s32[24,64]{1,0:T(8,128)} %pos_ref.1, ...), custom_call_target="tpu_custom_call" | custom-call | tf_op jit(solution)/shard_map/fill_caches/pallas_call | solution.py:525
  33.3 107.1 %attend_and_combine.1 = bf16[24,64,2048]{2,1,0:T(8,128)(2,1)S(1)} custom-call(s32[24]{0:T(128)} %ctx_ref.3, bf16[2048]{0:T(1024)(128)(2,1)} %gain_ref.3, bf16[3,4,4,64,256]{4,3,2,1,0:T(8,128)(2,1)} %get-tuple-element.8.q_hbm, f32[12,2,32,128]{3,2,1,0:T(8,128)} %get-tuple-element.9.tab_hbm, f32[4,264,256]{2,1,0:T(8,128)} %get-tuple-element.10.msg_hbm, ...), custom_call_target="tpu_custom_call" | custom-call | tf_op jit(solution)/shard_map/attend_and_combine/pallas_call | solution.py:552
  140.4 2.7 %copy.18 = bf16[24,64,2048]{2,1,0:T(8,128)(2,1)} copy(bf16[24,64,2048]{2,1,0:T(8,128)(2,1)S(1)} %attend_and_combine.1) | data formatting | bytes 12582912

commit v5 on v4

--- a/solution.py
+++ b/solution.py
@@ -17,7 +17,6 @@
 BF16 = jnp.bfloat16
 CHUNK = 4
 EARLY_CHUNKS = 3
-HEAD_STEPS = 3
 
 SCHEDULE = (
     ('emit', 0, (29, 31, 35, 36, 37, 38)),
@@ -144,117 +143,108 @@
                  q_ref, tab_ref, msg_hbm, ko_hbm, vo_hbm,
                  buf, xbuf, new_ref, wk_ref, wv_ref, wq_ref, vbuf, kext, qext, scores, msg, in_sem, out_sem, w_sem, msg_sem):
     cp_rank, cp_size = lax.axis_index('cp'), lax.axis_size('cp')
-    slots, _, per, num_blocks, kv_heads, hd, blk = buf.shape
-    nreq, tree = pos_ref.shape
-    steps = nreq // per
+    chunks, _, per, num_blocks, kv_heads, hd, blk = buf.shape
+    tree = pos_ref.shape[1]
     group = q_ref.shape[4] // tree
     width = x_hbm.shape[2]
     half = hd // 2
     cols = per * tree
 
-    def pair_of(idx):
-        return (idx + steps - HEAD_STEPS) % steps
-
-    def fetch(idx):
-        rows, to = pl.ds(pair_of(idx) * per, per), idx % slots
-        return [pltpu.make_async_copy(x_hbm.at[rows], xbuf.at[to], in_sem.at[to, 2])] + [
-            pltpu.make_async_copy(src.at[rows], buf.at[to, n], in_sem.at[to, n]) for n, src in enumerate((kc_hbm, vc_hbm))]
-
-    def flush(idx):
-        rows, frm = pl.ds(pair_of(idx) * per, per), idx % slots
-        return [pltpu.make_async_copy(buf.at[frm, n], dst.at[rows], out_sem.at[frm, n]) for n, dst in enumerate((ko_hbm, vo_hbm))]
+    def rows_of(c):
+        return pl.ds(c * per, per)
+
+    def fetch_rows(c):
+        return pltpu.make_async_copy(x_hbm.at[rows_of(c)], xbuf.at[c], in_sem.at[c, 2])
+
+    def fetch(c):
+        return [pltpu.make_async_copy(src.at[rows_of(c)], buf.at[c, n], in_sem.at[c, n]) for n, src in enumerate((kc_hbm, vc_hbm))]
+
+    def flush(c):
+        return [pltpu.make_async_copy(buf.at[c, n], dst.at[rows_of(c)], out_sem.at[c, n]) for n, dst in enumerate((ko_hbm, vo_hbm))]
 
     kv_weights = [pltpu.make_async_copy(src, dst, w_sem.at[n]) for n, (src, dst) in enumerate(((wk_hbm, wk_ref), (wv_hbm, wv_ref)))]
     q_weight = pltpu.make_async_copy(wq_hbm, wq_ref, w_sem.at[2])
-    ahead = slots // 2
-    for c in fetch(0) + kv_weights:
+    for c in [fetch_rows(0)] + kv_weights + fetch(0) + [q_weight]:
         c.start()
-    for idx in range(1, ahead):
-        for c in fetch(idx):
+    for n in range(1, chunks):
+        for c in [fetch_rows(n)] + fetch(n):
             c.start()
-    q_weight.start()
     prepare(vbuf, qext, hd, tree)
     diag = lax.broadcasted_iota(jnp.int32, (half, half), 0) == lax.broadcasted_iota(jnp.int32, (half, half), 1)
     freq = jnp.sum(jnp.where(diag, freq_ref[...][None, :], 0.0), axis=1, keepdims=True)
     for c in kv_weights:
         c.wait()
 
-    @pl.loop(0, steps)
-    def _(step):
-        slot, pair = step % slots, pair_of(step)
-        later = step + ahead
-
-        @pl.when(later < steps)
-        def _():
-            @pl.when(later >= slots)
-            def _():
-                for c in flush(later - slots):
-                    c.wait()
-
-            for c in fetch(later):
+    @pl.loop(0, chunks + EARLY_CHUNKS - 1)
+    def _(turn):
+        again = turn >= chunks
+        k = turn - jnp.where(again, chunks - 1, 0)
+
+        @pl.when(turn < chunks)
+        def _():
+            fetch_rows(k).wait()
+
+        h = normed_rows(xbuf[k].reshape(cols, width), gain_ref[...])
+        pos = jnp.concatenate([pos_ref[pl.ds(k * per + i, 1), :] for i in range(per)], axis=1).astype(F32)
+        cos, sin = cos_sin(pos * freq)
+
+        @pl.when(turn < chunks)
+        def _():
+            tab_ref[k, 0] = cos
+            tab_ref[k, 1] = sin
+            key_t = mm(h, wk_ref[...]).T
+            for n in range(kv_heads):
+                new_ref[0, n * hd:(n + 1) * hd, :] = rotate(key_t[n * hd:(n + 1) * hd], cos, sin).astype(BF16)
+            new_ref[1] = mm(h, wv_ref[...]).T.astype(BF16)
+            for c in fetch(k):
+                c.wait()
+            for i in range(per):
+                ctx = ctx_ref[k * per + i]
+                for j in range(num_blocks // 2, num_blocks):
+                    first_pos = (j * cp_size + cp_rank) * blk
+
+                    @pl.when((first_pos < ctx + tree) & (first_pos + blk > ctx))
+                    def _():
+                        tok = first_pos - ctx + lax.broadcasted_iota(jnp.int32, (cols, blk), 1)
+                        row = lax.broadcasted_iota(jnp.int32, (cols, blk), 0) - i * tree
+                        pick = jnp.where((row == tok) & (row >= 0) & (row < tree), 1.0, 0.0).astype(BF16)
+                        tok_h = first_pos - ctx + lax.broadcasted_iota(jnp.int32, (hd, blk), 1)
+                        fresh = (tok_h >= 0) & (tok_h < tree)
+                        for n in range(2):
+                            put = mm(new_ref[n], pick)
+                            for head in range(kv_heads):
+                                old = buf[k, n, i, j, head].astype(F32)
+                                buf[k, n, i, j, head] = jnp.where(fresh, put[head * hd:(head + 1) * hd], old).astype(BF16)
+
+            for c in flush(k):
                 c.start()
 
-        for c in fetch(step):
-            c.wait()
-        h = normed_rows(xbuf[slot].reshape(cols, width), gain_ref[...])
-        pos = jnp.concatenate([pos_ref[pl.ds(pair * per + i, 1), :] for i in range(per)], axis=1).astype(F32)
-        cos, sin = cos_sin(pos * freq)
-        tab_ref[pair, 0] = cos
-        tab_ref[pair, 1] = sin
-        key_t = mm(h, wk_ref[...]).T
-        for n in range(kv_heads):
-            new_ref[0, n * hd:(n + 1) * hd, :] = rotate(key_t[n * hd:(n + 1) * hd], cos, sin).astype(BF16)
-        new_ref[1] = mm(h, wv_ref[...]).T.astype(BF16)
-        for i in range(per):
-            ctx = ctx_ref[pair * per + i]
-            for j in range(num_blocks // 2, num_blocks):
-                first_pos = (j * cp_size + cp_rank) * blk
-
-                @pl.when((first_pos < ctx + tree) & (first_pos + blk > ctx))
-                def _():
-                    tok = first_pos - ctx + lax.broadcasted_iota(jnp.int32, (cols, blk), 1)
-                    row = lax.broadcasted_iota(jnp.int32, (cols, blk), 0) - i * tree
-                    pick = jnp.where((row == tok) & (row >= 0) & (row < tree), 1.0, 0.0).astype(BF16)
-                    tok_h = first_pos - ctx + lax.broadcasted_iota(jnp.int32, (hd, blk), 1)
-                    fresh = (tok_h >= 0) & (tok_h < tree)
-                    for n in range(2):
-                        put = mm(new_ref[n], pick)
-                        for head in range(kv_heads):
-                            old = buf[slot, n, i, j, head].astype(F32)
-                            buf[slot, n, i, j, head] = jnp.where(fresh, put[head * hd:(head + 1) * hd], old).astype(BF16)
-
-        for c in flush(step):
-            c.start()
-
-        @pl.when(step == HEAD_STEPS)
+        @pl.when(turn == 0)
         def _():
             q_weight.wait()
 
-        @pl.when(pair < EARLY_CHUNKS * CHUNK // per)
-        def _():
-            req = pair * per
-
+        @pl.when((turn == 0) | (turn >= chunks))
+        def _():
             def out(i, head, value):
-                q_ref[req // CHUNK, req % CHUNK + i, head] = value
+                q_ref[k, i, head] = value
 
             project_queries(h, wq_ref, cos, sin, out, hd, group, tree)
 
-        @pl.when(pair < CHUNK // per)
+        @pl.when(turn == 0)
         def _():
             @pl.loop(0, per)
             def _(i):
-                req = pair * per + i
                 for j in range(num_blocks):
                     for head in range(kv_heads):
-                        vbuf[j, head, :hd, :] = buf[slot, 1, i, j, head]
-                attention(ctx_ref[req], mask_ref[req], q_ref.at[0, req], buf.at[slot, 0, i], vbuf, kext, qext, scores, msg.at[req], cp_rank)
-                pltpu.make_async_copy(msg.at[req], msg_hbm.at[req], msg_sem.at[req]).start()
-
-    for idx in range(steps - slots, steps):
-        for c in flush(idx):
+                        vbuf[j, head, :hd, :] = buf[0, 1, i, j, head]
+                attention(ctx_ref[i], mask_ref[i], q_ref.at[0, i], buf.at[0, 0, i], vbuf, kext, qext, scores, msg.at[i], cp_rank)
+                pltpu.make_async_copy(msg.at[i], msg_hbm.at[i], msg_sem.at[i]).start()
+
+    for i in range(per):
+        pltpu.make_async_copy(msg.at[i], msg_hbm.at[i], msg_sem.at[i]).wait()
+    for n in range(chunks):
+        for c in flush(n):
             c.wait()
-    for req in range(CHUNK):
-        pltpu.make_async_copy(msg.at[req], msg_hbm.at[req], msg_sem.at[req]).wait()
 
 
 def attend_kernel(ctx_ref, gain_ref, q_hbm, tab_hbm, msg_hbm, mask_hbm, kc_hbm, vc_hbm, hid_hbm, wq_hbm, wo_hbm, out_ref,
@@ -516,8 +506,7 @@
         vmem = pl.BlockSpec(memory_space=pltpu.VMEM)
         smem = pl.BlockSpec(memory_space=pltpu.SMEM)
         cache_shape = jax.ShapeDtypeStruct(keys.shape, BF16)
-        per, slots = CHUNK // 2, 8
-        steps, rows = nreq // per, per * tree
+        rows = CHUNK * tree
         qcols = group * tree
         rows_msg = kv_heads * hd + 2 * kv_heads
         ext = hd + tree + 16
@@ -526,11 +515,11 @@
             cache_kernel,
             in_specs=[smem] + [vmem] * 4 + [hbm] * 6,
             out_specs=[vmem, vmem, hbm, hbm, hbm],
-            out_shape=[jax.ShapeDtypeStruct((EARLY_CHUNKS, CHUNK, kv_heads, hd, qcols), BF16), jax.ShapeDtypeStruct((steps, 2, hd // 2, rows), F32),
+            out_shape=[jax.ShapeDtypeStruct((EARLY_CHUNKS, CHUNK, kv_heads, hd, qcols), BF16), jax.ShapeDtypeStruct((chunks, 2, hd // 2, rows), F32),
                        jax.ShapeDtypeStruct((CHUNK, rows_msg, qcols), F32), cache_shape, cache_shape],
             scratch_shapes=[
-                pltpu.VMEM((slots, 2, per, num_blocks, kv_heads, hd, blk), BF16),
-                pltpu.VMEM((slots, per, tree, width), BF16),
+                pltpu.VMEM((chunks, 2, CHUNK, num_blocks, kv_heads, hd, blk), BF16),
+                pltpu.VMEM((chunks, CHUNK, tree, width), BF16),
                 pltpu.VMEM((2, kvdim, rows), BF16),
                 pltpu.VMEM((width, kvdim), BF16),
                 pltpu.VMEM((width, kvdim), BF16),
@@ -540,8 +529,8 @@
                 pltpu.VMEM((kv_heads, ext, qcols), BF16),
                 pltpu.VMEM((2, num_blocks * blk, qcols), F32),
                 pltpu.VMEM((CHUNK, rows_msg, qcols), F32),
-                pltpu.SemaphoreType.DMA((slots, 3)),
-                pltpu.SemaphoreType.DMA((slots, 2)),
+                pltpu.SemaphoreType.DMA((chunks, 3)),
+                pltpu.SemaphoreType.DMA((chunks, 2)),
                 pltpu.SemaphoreType.DMA((3,)),
                 pltpu.SemaphoreType.DMA((CHUNK,)),
             ],
@@ -572,7 +561,7 @@
                 pltpu.VMEM(wide_rows, BF16),
                 pltpu.VMEM((width, qdim), BF16),
                 pltpu.VMEM((CHUNK, tree, width), BF16),
-                pltpu.VMEM((CHUNK // per, 2, hd // 2, rows), F32),
+                pltpu.VMEM((1, 2, hd // 2, rows), F32),
                 pltpu.VMEM((EARLY_CHUNKS, CHUNK, kv_heads, hd, qcols), BF16),
                 pltpu.SemaphoreType.DMA((2, 3)),
                 pltpu.SemaphoreType.DMA((group, kv_heads)),

time: 143 us -> 146 us (1.021)
  Pallas kernels: 140 us -> 142 us
    pallas_call x1, Pallas kernels: 32.6 us -> 36 us  [local_step(): pl.pallas_call(cache_kernel, in_specs=[smem] + [vmem] * 4 + [hbm] * 6, ou...]
where the time goes in v5:
time: 146 us
  Pallas kernels  142 us (97%)
  local copies, waits for them, and re-layouts  2.71 us (2%)
    pallas_call x1, Pallas kernels, local_step(): pl.pallas_call(attend_kernel, in_specs=[smem, vmem] + [hbm] * 9, out_spec...  106 us
    pallas_call x1, Pallas kernels, local_step(): pl.pallas_call(cache_kernel, in_specs=[smem] + [vmem] * 4 + [hbm] * 6, ou...  36 us

profile of v5, /device:TPU:0, one launch (start us, length us, event | category | flops | bytes accessed | tf_op | source)
XLA Modules:
  0.0 145.6 jit_solution(5627612471224547647)
XLA Ops:
  0.6 36.0 %fill_caches.1 = (bf16[3,4,4,64,256]{4,3,2,1,0:T(8,128)(2,1)}, f32[6,2,32,256]{3,2,1,0:T(8,128)}, f32[4,264,256]{2,1,0:T(8,128)}, bf16[24,4,4,64,256]{4,3,2,1,0:T(8,128)(2,1)}, bf16[24,4,4,64,256]{4,3,2,1,0:T(8,128)(2,1)}) custom-call(s32[24]{0:T(128)} %ctx_ref.3, bf16[2048]{0:T(1024)(128)(2,1)} %gain_ref.3, s32[24,64]{1,0:T(8,128)} %pos_ref.1, ...), custom_call_target="tpu_custom_call" | custom-call | tf_op jit(solution)/shard_map/fill_caches/pallas_call | solution.py:514
  36.6 106.3 %attend_and_combine.1 = bf16[24,64,2048]{2,1,0:T(8,128)(2,1)S(1)} custom-call(s32[24]{0:T(128)} %ctx_ref.3, bf16[2048]{0:T(1024)(128)(2,1)} %gain_ref.3, bf16[3,4,4,64,256]{4,3,2,1,0:T(8,128)(2,1)} %get-tuple-element.8.q_hbm, f32[6,2,32,256]{3,2,1,0:T(8,128)} %get-tuple-element.9.tab_hbm, f32[4,264,256]{2,1,0:T(8,128)} %get-tuple-element.10.msg_hbm, ...), custom_call_target="tpu_custom_call" | custom-call | tf_op jit(solution)/shard_map/attend_and_combine/pallas_call | solution.py:541
  142.9 2.7 %copy.18 = bf16[24,64,2048]{2,1,0:T(8,128)(2,1)} copy(bf16[24,64,2048]{2,1,0:T(8,128)(2,1)S(1)} %attend_and_combine.1) | data formatting | bytes 12582912

commit v6 on v5

--- a/solution.py
+++ b/solution.py
@@ -164,16 +164,15 @@
 
     kv_weights = [pltpu.make_async_copy(src, dst, w_sem.at[n]) for n, (src, dst) in enumerate(((wk_hbm, wk_ref), (wv_hbm, wv_ref)))]
     q_weight = pltpu.make_async_copy(wq_hbm, wq_ref, w_sem.at[2])
-    for c in [fetch_rows(0)] + kv_weights + fetch(0) + [q_weight]:
+    for c in [fetch_rows(0)] + kv_weights:
         c.start()
-    for n in range(1, chunks):
-        for c in [fetch_rows(n)] + fetch(n):
-            c.start()
     prepare(vbuf, qext, hd, tree)
     diag = lax.broadcasted_iota(jnp.int32, (half, half), 0) == lax.broadcasted_iota(jnp.int32, (half, half), 1)
     freq = jnp.sum(jnp.where(diag, freq_ref[...][None, :], 0.0), axis=1, keepdims=True)
     for c in kv_weights:
         c.wait()
+    for c in fetch(0) + [q_weight]:
+        c.start()
 
     @pl.loop(0, chunks + EARLY_CHUNKS - 1)
     def _(turn):
@@ -222,6 +221,9 @@
         @pl.when(turn == 0)
         def _():
             q_weight.wait()
+            for n in range(1, chunks):
+                for c in [fetch_rows(n)] + fetch(n):
+                    c.start()
 
         @pl.when((turn == 0) | (turn >= chunks))
         def _():
@@ -316,8 +318,6 @@
 
     for n in range(CHUNK):
         share(0, (2 * (1 - chip) + n) % CHUNK, n // 2)
-    for c in weight_copies() + resid_copies() + chunk_copies(EARLY_CHUNKS) + [query_weight]:
-        c.start()
     first_queries.wait()
 
     def queries(k):
@@ -474,6 +474,16 @@
         @pl.when(n < nreq)
         def _():
             attend(n)
+
+        @pl.when(n == CHUNK)
+        def _():
+            for c in weight_copies() + resid_copies():
+                c.start()
+
+        @pl.when(n == CHUNK + 1)
+        def _():
+            for c in chunk_copies(EARLY_CHUNKS) + [query_weight]:
+                c.start()
 
         for name, lowest, turns in SCHEDULE:
             @pl.when(functools.reduce(jnp.logical_or, [n == t for t in turns]))

time: 146 us -> 140 us (0.959)
  Pallas kernels: 142 us -> 136 us
    pallas_call x1, Pallas kernels: 36 us -> 30.1 us  [local_step(): pl.pallas_call(cache_kernel, in_specs=[smem] + [vmem] * 4 + [hbm] * 6, ou...]
where the time goes in v6:
time: 140 us
  Pallas kernels  136 us (97%)
  local copies, waits for them, and re-layouts  2.71 us (2%)
    pallas_call x1, Pallas kernels, local_step(): pl.pallas_call(attend_kernel, in_specs=[smem, vmem] + [hbm] * 9, out_spec...  106 us
    pallas_call x1, Pallas kernels, local_step(): pl.pallas_call(cache_kernel, in_specs=[smem] + [vmem] * 4 + [hbm] * 6, ou...  30.1 us

profile of v6, /device:TPU:0, one launch (start us, length us, event | category | flops | bytes accessed | tf_op | source)
XLA Modules:
  0.0 139.8 jit_solution(6206895445280865609)
XLA Ops:
  0.6 30.1 %fill_caches.1 = (bf16[3,4,4,64,256]{4,3,2,1,0:T(8,128)(2,1)}, f32[6,2,32,256]{3,2,1,0:T(8,128)}, f32[4,264,256]{2,1,0:T(8,128)}, bf16[24,4,4,64,256]{4,3,2,1,0:T(8,128)(2,1)}, bf16[24,4,4,64,256]{4,3,2,1,0:T(8,128)(2,1)}) custom-call(s32[24]{0:T(128)} %ctx_ref.3, bf16[2048]{0:T(1024)(128)(2,1)} %gain_ref.3, s32[24,64]{1,0:T(8,128)} %pos_ref.1, ...), custom_call_target="tpu_custom_call" | custom-call | tf_op jit(solution)/shard_map/fill_caches/pallas_call | solution.py:524
  30.7 106.4 %attend_and_combine.1 = bf16[24,64,2048]{2,1,0:T(8,128)(2,1)S(1)} custom-call(s32[24]{0:T(128)} %ctx_ref.3, bf16[2048]{0:T(1024)(128)(2,1)} %gain_ref.3, bf16[3,4,4,64,256]{4,3,2,1,0:T(8,128)(2,1)} %get-tuple-element.8.q_hbm, f32[6,2,32,256]{3,2,1,0:T(8,128)} %get-tuple-element.9.tab_hbm, f32[4,264,256]{2,1,0:T(8,128)} %get-tuple-element.10.msg_hbm, ...), custom_call_target="tpu_custom_call" | custom-call | tf_op jit(solution)/shard_map/attend_and_combine/pallas_call | solution.py:551
  137.1 2.7 %copy.18 = bf16[24,64,2048]{2,1,0:T(8,128)(2,1)} copy(bf16[24,64,2048]{2,1,0:T(8,128)(2,1)S(1)} %attend_and_combine.1) | data formatting | bytes 12582912

commit v7 on v6

--- a/solution.py
+++ b/solution.py
@@ -16,16 +16,15 @@
 F32 = jnp.float32
 BF16 = jnp.bfloat16
 CHUNK = 4
-EARLY_CHUNKS = 3
 
 SCHEDULE = (
-    ('emit', 0, (29, 31, 35, 36, 37, 38)),
-    ('diagonal', 0, (22, 29, 30, 33, 34, 35)),
-    ('forward', 0, (15, 17, 26, 30, 31, 32)),
-    ('project', 0, (9, 10, 17, 19, 24, 25)),
-    ('query', EARLY_CHUNKS, (9, 14, 16)),
-    ('merge', 0, (4, 7, 9, 15, 19, 21)),
-    ('finish', 0, (10, 13, 21, 24, 27, 28)),
+    ('finish', 0, (7, 14, 17, 25, 26, 27)),
+    ('query', 2, (3, 7, 11, 15)),
+    ('forward', 0, (11, 22, 23, 27, 28, 29)),
+    ('merge', 1, (3, 6, 10, 15, 18)),
+    ('project', 0, (3, 7, 11, 15, 20, 24)),
+    ('diagonal', 0, (18, 25, 26, 29, 31, 32)),
+    ('emit', 0, (23, 28, 29, 30, 32, 33)),
 )
 
 def mm(a, b):
@@ -145,7 +144,7 @@
     cp_rank, cp_size = lax.axis_index('cp'), lax.axis_size('cp')
     chunks, _, per, num_blocks, kv_heads, hd, blk = buf.shape
     tree = pos_ref.shape[1]
-    group = q_ref.shape[4] // tree
+    group = q_ref.shape[3] // tree
     width = x_hbm.shape[2]
     half = hd // 2
     cols = per * tree
@@ -174,75 +173,64 @@
     for c in fetch(0) + [q_weight]:
         c.start()
 
-    @pl.loop(0, chunks + EARLY_CHUNKS - 1)
-    def _(turn):
-        again = turn >= chunks
-        k = turn - jnp.where(again, chunks - 1, 0)
-
-        @pl.when(turn < chunks)
-        def _():
-            fetch_rows(k).wait()
-
+    @pl.loop(0, chunks)
+    def _(k):
+        fetch_rows(k).wait()
         h = normed_rows(xbuf[k].reshape(cols, width), gain_ref[...])
         pos = jnp.concatenate([pos_ref[pl.ds(k * per + i, 1), :] for i in range(per)], axis=1).astype(F32)
         cos, sin = cos_sin(pos * freq)
 
-        @pl.when(turn < chunks)
-        def _():
-            tab_ref[k, 0] = cos
-            tab_ref[k, 1] = sin
-            key_t = mm(h, wk_ref[...]).T
-            for n in range(kv_heads):
-                new_ref[0, n * hd:(n + 1) * hd, :] = rotate(key_t[n * hd:(n + 1) * hd], cos, sin).astype(BF16)
-            new_ref[1] = mm(h, wv_ref[...]).T.astype(BF16)
-            for c in fetch(k):
-                c.wait()
-            for i in range(per):
-                ctx = ctx_ref[k * per + i]
-                for j in range(num_blocks // 2, num_blocks):
-                    first_pos = (j * cp_size + cp_rank) * blk
-
-                    @pl.when((first_pos < ctx + tree) & (first_pos + blk > ctx))
-                    def _():
-                        tok = first_pos - ctx + lax.broadcasted_iota(jnp.int32, (cols, blk), 1)
-                        row = lax.broadcasted_iota(jnp.int32, (cols, blk), 0) - i * tree
-                        pick = jnp.where((row == tok) & (row >= 0) & (row < tree), 1.0, 0.0).astype(BF16)
-                        tok_h = first_pos - ctx + lax.broadcasted_iota(jnp.int32, (hd, blk), 1)
-                        fresh = (tok_h >= 0) & (tok_h < tree)
-                        for n in range(2):
-                            put = mm(new_ref[n], pick)
-                            for head in range(kv_heads):
-                                old = buf[k, n, i, j, head].astype(F32)
-                                buf[k, n, i, j, head] = jnp.where(fresh, put[head * hd:(head + 1) * hd], old).astype(BF16)
-
-            for c in flush(k):
-                c.start()
-
-        @pl.when(turn == 0)
+        tab_ref[k, 0] = cos
+        tab_ref[k, 1] = sin
+        key_t = mm(h, wk_ref[...]).T
+        for n in range(kv_heads):
+            new_ref[0, n * hd:(n + 1) * hd, :] = rotate(key_t[n * hd:(n + 1) * hd], cos, sin).astype(BF16)
+        new_ref[1] = mm(h, wv_ref[...]).T.astype(BF16)
+        for c in fetch(k):
+            c.wait()
+        for i in range(per):
+            ctx = ctx_ref[k * per + i]
+            for j in range(num_blocks // 2, num_blocks):
+                first_pos = (j * cp_size + cp_rank) * blk
+
+                @pl.when((first_pos < ctx + tree) & (first_pos + blk > ctx))
+                def _():
+                    tok = first_pos - ctx + lax.broadcasted_iota(jnp.int32, (cols, blk), 1)
+                    row = lax.broadcasted_iota(jnp.int32, (cols, blk), 0) - i * tree
+                    pick = jnp.where((row == tok) & (row >= 0) & (row < tree), 1.0, 0.0).astype(BF16)
+                    tok_h = first_pos - ctx + lax.broadcasted_iota(jnp.int32, (hd, blk), 1)
+                    fresh = (tok_h >= 0) & (tok_h < tree)
+                    for n in range(2):
+                        put = mm(new_ref[n], pick)
+                        for head in range(kv_heads):
+                            old = buf[k, n, i, j, head].astype(F32)
+                            buf[k, n, i, j, head] = jnp.where(fresh, put[head * hd:(head + 1) * hd], old).astype(BF16)
+
+        for c in flush(k):
+            c.start()
+
+        @pl.when(k == 0)
         def _():
             q_weight.wait()
             for n in range(1, chunks):
                 for c in [fetch_rows(n)] + fetch(n):
                     c.start()
 
-        @pl.when((turn == 0) | (turn >= chunks))
-        def _():
             def out(i, head, value):
-                q_ref[k, i, head] = value
+                q_ref[i, head] = value
 
             project_queries(h, wq_ref, cos, sin, out, hd, group, tree)
 
-        @pl.when(turn == 0)
-        def _():
-            @pl.loop(0, per)
+            @pl.loop(0, per // 2)
             def _(i):
+                req = (1 - cp_rank // 2) * (per // 2) + i
                 for j in range(num_blocks):
                     for head in range(kv_heads):
-                        vbuf[j, head, :hd, :] = buf[0, 1, i, j, head]
-                attention(ctx_ref[i], mask_ref[i], q_ref.at[0, i], buf.at[0, 0, i], vbuf, kext, qext, scores, msg.at[i], cp_rank)
+                        vbuf[j, head, :hd, :] = buf[0, 1, req, j, head]
+                attention(ctx_ref[req], mask_ref[req], q_ref.at[req], buf.at[0, 0, req], vbuf, kext, qext, scores, msg.at[i], cp_rank)
                 pltpu.make_async_copy(msg.at[i], msg_hbm.at[i], msg_sem.at[i]).start()
 
-    for i in range(per):
+    for i in range(per // 2):
         pltpu.make_async_copy(msg.at[i], msg_hbm.at[i], msg_sem.at[i]).wait()
     for n in range(chunks):
         for c in flush(n):
@@ -257,7 +245,7 @@
     partner = {'cp': chip * 2 + 1 - core}
     across_x = {'cp': (1 - chip) * 2 + core}
     across_y = {'tp': 1 - tp}
-    _, _, heads, hd, qcols = q_hbm.shape
+    _, heads, hd, qcols = q_hbm.shape
     nreq = mask_hbm.shape[0]
     tree = mask_hbm.shape[1]
     group = qcols // tree
@@ -276,11 +264,16 @@
     for to in (partner, across_x, across_y):
         pl.semaphore_signal(barrier, inc=1, device_id=to, device_id_type=MESH)
 
-    def request_of(n):
-        return (n // CHUNK) * CHUNK + (2 * (1 - chip) + n % CHUNK) % CHUNK
+    turns = nreq - CHUNK // 2
+
+    def turn_of(n):
+        pair = n // 2
+        foreign = jnp.where((pair % 2 == 0) & (n < turns - 2), 1, 0)
+        return pair // 2 + foreign, 2 * (chip + foreign - 2 * chip * foreign) + n % 2, foreign
 
     def fetch(n):
-        r, to = request_of(n), n % 2
+        k, i, _ = turn_of(n)
+        r, to = k * CHUNK + i, n % 2
         return [pltpu.make_async_copy(kc_hbm.at[r], kbuf.at[to], kv_sem.at[to, 0]),
                 pltpu.make_async_copy(vc_hbm.at[r], vbuf.at[to, :, :, pl.ds(0, hd), :], kv_sem.at[to, 1]),
                 pltpu.make_async_copy(mask_hbm.at[r], mbuf.at[to], kv_sem.at[to, 2])]
@@ -295,7 +288,7 @@
     def resid_copies():
         return [pltpu.make_async_copy(hid_hbm.at[k * CHUNK + cp, :, own_cols], resid.at[k], hid_sem.at[k]) for k in range(chunks)]
 
-    first_queries = pltpu.make_async_copy(q_hbm, qbuf, q_sem.at[0])
+    first_queries = pltpu.make_async_copy(q_hbm, qbuf.at[0], q_sem.at[0])
     query_weight = pltpu.make_async_copy(wq_hbm, wq_ref, q_sem.at[1])
 
     def chunk_copies(k):
@@ -303,8 +296,8 @@
         return [pltpu.make_async_copy(hid_hbm.at[pl.ds(k * CHUNK, CHUNK)], xbuf, q_sem.at[2]),
                 pltpu.make_async_copy(tab_hbm.at[pl.ds(k * pairs, pairs)], tbuf, q_sem.at[3])]
 
-    first_msgs = pltpu.make_async_copy(msg_hbm, msg.at[0], q_sem.at[4])
-    for c in [first_msgs] + fetch(CHUNK) + [first_queries]:
+    first_msgs = pltpu.make_async_copy(msg_hbm, msg.at[0, pl.ds(2 * (1 - chip), 2)], q_sem.at[4])
+    for c in [first_msgs] + chunk_copies(1) + [query_weight] + fetch(0) + [first_queries]:
         c.start()
     for to in range(2):
         prepare(vbuf.at[to], qext, hd, tree)
@@ -316,15 +309,14 @@
         def _():
             remote(msg.at[k, i], rpart.at[k, which], k, which, partner).start()
 
-    for n in range(CHUNK):
-        share(0, (2 * (1 - chip) + n) % CHUNK, n // 2)
-    first_queries.wait()
+    for n in range(2):
+        share(0, 2 * (1 - chip) + n, 0)
 
     def queries(k):
         for c in chunk_copies(k):
             c.wait()
 
-        @pl.when(k == EARLY_CHUNKS)
+        @pl.when(k == 1)
         def _():
             query_weight.wait()
 
@@ -333,7 +325,7 @@
         sin = jnp.concatenate([tbuf[p, 1] for p in range(tbuf.shape[0])], axis=1)
 
         def out(i, head, value):
-            qbuf[k % EARLY_CHUNKS, i, head] = value
+            qbuf[k % 2, i, head] = value
 
         project_queries(h, wq_ref, cos, sin, out, hd, group, tree)
 
@@ -343,10 +335,10 @@
                 c.start()
 
     def attend(n):
-        k, r, slot = n // CHUNK, request_of(n), n % 2
-        i = r - k * CHUNK
-
-        @pl.when(n + 1 < nreq)
+        k, i, foreign = turn_of(n)
+        r, slot = k * CHUNK + i, n % 2
+
+        @pl.when(n + 1 < turns)
         def _():
             for c in fetch(n + 1):
                 c.start()
@@ -354,9 +346,9 @@
         ctx = ctx_ref[r]
         for c in fetch(n):
             c.wait()
-        attention(ctx, mbuf[slot], qbuf.at[k % EARLY_CHUNKS, i], kbuf.at[slot], vbuf.at[slot], kext, qext, scores, msg.at[k, i], cp)
-
-        share(k, i, (n % CHUNK) // 2)
+        attention(ctx, mbuf[slot], qbuf.at[k % 2, i], kbuf.at[slot], vbuf.at[slot], kext, qext, scores, msg.at[k, i], cp)
+
+        share(k, i, 1 - foreign)
 
     stat = heads * hd
 
@@ -469,26 +461,25 @@
 
     work = {'merge': merge_chip, 'query': queries, 'project': project, 'finish': finish, 'forward': forward, 'diagonal': forward_diagonal, 'emit': emit}
 
-    @pl.loop(CHUNK, 1 + max(max(turns) for _, _, turns in SCHEDULE))
+    merge_chip(0)
+    queries(1)
+    first_queries.wait()
+
+    @pl.loop(0, 1 + max(max(when) for _, _, when in SCHEDULE))
     def _(n):
-        @pl.when(n < nreq)
+        @pl.when(n < turns)
         def _():
             attend(n)
 
-        @pl.when(n == CHUNK)
+        @pl.when(n == 0)
         def _():
             for c in weight_copies() + resid_copies():
                 c.start()
 
-        @pl.when(n == CHUNK + 1)
-        def _():
-            for c in chunk_copies(EARLY_CHUNKS) + [query_weight]:
-                c.start()
-
-        for name, lowest, turns in SCHEDULE:
-            @pl.when(functools.reduce(jnp.logical_or, [n == t for t in turns]))
+        for name, lowest, when in SCHEDULE:
+            @pl.when(functools.reduce(jnp.logical_or, [n == t for t in when]))
             def _():
-                work[name](sum([jnp.where(n > t, 1, 0) for t in turns]) + lowest)
+                work[name](sum([jnp.where(n > t, 1, 0) for t in when]) + lowest)
 
     @pl.loop(0, chunks)
     def _(k):
@@ -525,8 +516,8 @@
             cache_kernel,
             in_specs=[smem] + [vmem] * 4 + [hbm] * 6,
             out_specs=[vmem, vmem, hbm, hbm, hbm],
-            out_shape=[jax.ShapeDtypeStruct((EARLY_CHUNKS, CHUNK, kv_heads, hd, qcols), BF16), jax.ShapeDtypeStruct((chunks, 2, hd // 2, rows), F32),
-                       jax.ShapeDtypeStruct((CHUNK, rows_msg, qcols), F32), cache_shape, cache_shape],
+            out_shape=[jax.ShapeDtypeStruct((CHUNK, kv_heads, hd, qcols), BF16), jax.ShapeDtypeStruct((chunks, 2, hd // 2, rows), F32),
+                       jax.ShapeDtypeStruct((CHUNK // 2, rows_msg, qcols), F32), cache_shape, cache_shape],
             scratch_shapes=[
                 pltpu.VMEM((chunks, 2, CHUNK, num_blocks, kv_heads, hd, blk), BF16),
                 pltpu.VMEM((chunks, CHUNK, tree, width), BF16),
@@ -538,11 +529,11 @@
                 pltpu.VMEM((late_blocks, kv_heads, ext, blk), BF16),
                 pltpu.VMEM((kv_heads, ext, qcols), BF16),
                 pltpu.VMEM((2, num_blocks * blk, qcols), F32),
-                pltpu.VMEM((CHUNK, rows_msg, qcols), F32),
+                pltpu.VMEM((CHUNK // 2, rows_msg, qcols), F32),
                 pltpu.SemaphoreType.DMA((chunks, 3)),
                 pltpu.SemaphoreType.DMA((chunks, 2)),
                 pltpu.SemaphoreType.DMA((3,)),
-                pltpu.SemaphoreType.DMA((CHUNK,)),
+                pltpu.SemaphoreType.DMA((CHUNK // 2,)),
             ],
             compiler_params=pltpu.CompilerParams(vmem_limit_bytes=62 * 2**20),
             name='fill_caches',
@@ -572,7 +563,7 @@
                 pltpu.VMEM((width, qdim), BF16),
                 pltpu.VMEM((CHUNK, tree, width), BF16),
                 pltpu.VMEM((1, 2, hd // 2, rows), F32),
-                pltpu.VMEM((EARLY_CHUNKS, CHUNK, kv_heads, hd, qcols), BF16),
+                pltpu.VMEM((2, CHUNK, kv_heads, hd, qcols), BF16),
                 pltpu.SemaphoreType.DMA((2, 3)),
                 pltpu.SemaphoreType.DMA((group, kv_heads)),
                 pltpu.SemaphoreType.DMA((chunks,)),

time: 140 us -> 139 us (level)
    pallas_call x1, Pallas kernels: 30.1 us -> 23.4 us  [local_step(): pl.pallas_call(cache_kernel, in_specs=[smem] + [vmem] * 4 + [hbm] * 6, ou...]
    pallas_call x1, Pallas kernels: 106 us -> 112 us  [local_step(): pl.pallas_call(attend_kernel, in_specs=[smem, vmem] + [hbm] * 9, out_spec...]
where the time goes in v7:
time: 139 us; the launch traced here: 138 us
  Pallas kernels  135 us (97%)
  local copies, waits for them, and re-layouts  2.71 us (2%)
    pallas_call x1, Pallas kernels, local_step(): pl.pallas_call(attend_kernel, in_specs=[smem, vmem] + [hbm] * 9, out_spec...  112 us
    pallas_call x1, Pallas kernels, local_step(): pl.pallas_call(cache_kernel, in_specs=[smem] + [vmem] * 4 + [hbm] * 6, ou...  23.4 us

profile of v7, /device:TPU:0, one launch (start us, length us, event | category | flops | bytes accessed | tf_op | source)
XLA Modules:
  0.0 138.3 jit_solution(17294187608029910258)
XLA Ops:
  0.6 23.4 %fill_caches.1 = (bf16[4,4,64,256]{3,2,1,0:T(8,128)(2,1)}, f32[6,2,32,256]{3,2,1,0:T(8,128)}, f32[2,264,256]{2,1,0:T(8,128)}, bf16[24,4,4,64,256]{4,3,2,1,0:T(8,128)(2,1)}, bf16[24,4,4,64,256]{4,3,2,1,0:T(8,128)(2,1)}) custom-call(s32[24]{0:T(128)} %ctx_ref.3, bf16[2048]{0:T(1024)(128)(2,1)} %gain_ref.3, s32[24,64]{1,0:T(8,128)} %pos_ref.1, ...), custom_call_target="tpu_custom_call" | custom-call | tf_op jit(solution)/shard_map/fill_caches/pallas_call | solution.py:515
  24.0 111.6 %attend_and_combine.1 = bf16[24,64,2048]{2,1,0:T(8,128)(2,1)S(1)} custom-call(s32[24]{0:T(128)} %ctx_ref.3, bf16[2048]{0:T(1024)(128)(2,1)} %gain_ref.3, bf16[4,4,64,256]{3,2,1,0:T(8,128)(2,1)} %get-tuple-element.8.q_hbm, f32[6,2,32,256]{3,2,1,0:T(8,128)} %get-tuple-element.9.tab_hbm, f32[2,264,256]{2,1,0:T(8,128)} %get-tuple-element.10.msg_hbm, ...), custom_call_target="tpu_custom_call" | custom-call | tf_op jit(solution)/shard_map/attend_and_combine/pallas_call | solution.py:542
  135.6 2.7 %copy.18 = bf16[24,64,2048]{2,1,0:T(8,128)(2,1)} copy(bf16[24,64,2048]{2,1,0:T(8,128)(2,1)S(1)} %attend_and_combine.1) | data formatting | bytes 12582912
